TPU v7x, 32 devices: a whole 2x2x4 slice. The times are simulated.
32 devices in a mesh: data: 2 (over x), col: 4 (over z), row: 4 (over y, core).
Axes of the slice: x: 2, y: 2, z: 4, core: 2. Of those that a mesh axis runs over, the one named last changes fastest.
Arguments:
- image: bfloat16 [256, 128, 4], P(('data', 'row'), 'col'), parts along dimension 0
- w_enc1a: bfloat16 [3, 3, 4, 320], replicated
- b_enc1a: float32 [320], replicated
- w_enc1b: bfloat16 [3, 3, 320, 320], replicated
- b_enc1b: float32 [320], replicated
- w_enc2a: bfloat16 [3, 3, 320, 640], replicated
- b_enc2a: float32 [640], replicated
- w_enc2b: bfloat16 [3, 3, 640, 640], replicated
- b_enc2b: float32 [640], replicated
- w_mid_a: bfloat16 [3, 3, 640, 1280], replicated
- b_mid_a: float32 [1280], replicated
- w_mid_b: bfloat16 [3, 3, 1280, 1280], replicated
- b_mid_b: float32 [1280], replicated
- w_up2: bfloat16 [2, 2, 1280, 640], replicated
- w_dec2a: bfloat16 [3, 3, 1280, 640], replicated
- b_dec2a: float32 [640], replicated
- w_dec2b: bfloat16 [3, 3, 640, 640], replicated
- b_dec2b: float32 [640], replicated
- w_up1: bfloat16 [2, 2, 640, 320], replicated
- w_dec1a: bfloat16 [3, 3, 640, 320], replicated
- b_dec1a: float32 [320], replicated
- w_dec1b: bfloat16 [3, 3, 320, 320], replicated
- b_dec1b: float32 [320], replicated
- w_head: bfloat16 [320, 4], replicated
- b_head: float32 [4], replicated
Outputs:
- output: float32 [256, 128, 4], P(('data', 'row'), 'col'), parts along dimension 0
There are 2 independent parts. A program takes and returns all parts, laid end to end along the dimension named above; an argument that names none is the same for every part.
All inputs are finite; a program needn't handle non-finite values.
Results may differ from a plain program's by a relative error of at most 0.0170829.
Values are sent between devices in bfloat16 or wider.
A program may use at most 1 GiB of HBM per device.

v0:
```python
import jax
import jax.numpy as jnp
from jax import lax
from jax.experimental import pallas as pl
from jax.experimental.pallas import tpu as pltpu
from jax.sharding import PartitionSpec as P

F32 = jnp.float32
BF16 = jnp.bfloat16
STRIPS = 16
LAST = STRIPS - 1
SIDE = 4
SUB, LANE = 8, 128
TILE, HALF = 2 * LANE, LANE // 2
C1, C2, C3, C1P = 320, 640, 1280, 384
W3 = 32
END = SUB + TILE
MARGIN = END + SUB
TAPS = range(3)
TAP9 = 9
A_D2A = 17
A_REFILL = 27
A_D2B = 35
A_END = 44
B_END = 27
NOT = jnp.logical_not
AND = jnp.logical_and
OR = jnp.logical_or
RING_A = 18
RING_B = 10
MESH_ID = pl.DeviceIdType.MESH


def dot(lhs, rhs):
    return jnp.dot(lhs, rhs, preferred_element_type=F32)


def sum_of(parts):
    first, *rest = parts
    for part in rest:
        first = first + part
    return first


def relu(value):
    return jnp.maximum(value, 0.0)


def lane_mask(shape, below):
    return lax.broadcasted_iota(jnp.int32, shape, 1) < below


def column_index(rows, width):
    return lax.rem(lax.broadcasted_iota(jnp.int32, (rows, LANE), 0), width)


def kernel(x_ref, w_e1a, bias, w_head, h_e1b, h_e2a, h_e2b, h_ma, h_mb, h_up2, h_d2a, h_d2b, h_up1, h_d1a, h_d1b,
           out_ref,
           xb, xh, z, act1, s1, p1, act2, s2, p2, act3, mid, u2, act4, d2, u1, act5,
           v_e1b, v_d1a, v_d1b, v_up1, v_e2a, t_e1b, t_d1a, t_d1b, ring_a, ring_b,
           pm, pt, pl2, pl3, pool, up_f32, ys, ysend, yrecv,
           sem_w, sem_a, sem_b, x_send, x_recv, h_send, h_recv, e_send, e_recv, y_send, y_recv):
    col = lax.axis_index("col")
    row = lax.axis_index("row")
    data = lax.axis_index("data")

    def owner(strip):
        strip_col = strip // 4
        k = strip % 4
        return strip_col, k + (strip_col % 2) * (3 - 2 * k)

    def device(strip_col, strip_row):
        return (data, strip_col, strip_row)

    k_me = row + (col % 2) * (3 - 2 * row)
    me = 4 * col + k_me

    def whole(src, dst, index):
        return pltpu.make_async_copy(src, dst, sem_w.at[index])

    cp_e1b = whole(h_e1b, v_e1b, 0)
    cp_e2a = whole(h_e2a, v_e2a, 1)
    cp_up1 = whole(h_up1, v_up1, 2)
    cp_d1a = whole(h_d1a, v_d1a, 3)
    cp_d1b = whole(h_d1b, v_d1b, 4)

    def unit_a(unit):
        slot = unit % RING_A
        if unit < TAP9:
            src = h_e2b.at[unit]
        elif unit < A_D2A:
            src = h_up2.at[(unit - TAP9) // 2, pl.ds(((unit - TAP9) % 2) * C2, C2)]
        elif unit < A_D2B:
            local = unit - A_D2A
            dx, rest = local // 6, local % 6
            src = h_d2a.at[(rest // 2) * 3 + dx, pl.ds((rest % 2) * C2, C2)]
        else:
            local = unit - A_D2B
            src = h_d2b.at[(local % 3) * 3 + local // 3]
        return pltpu.make_async_copy(src, ring_a.at[slot], sem_a.at[slot])

    def wait_a(unit):
        slot = unit % RING_A
        pltpu.make_async_copy(h_e2b.at[0], ring_a.at[slot], sem_a.at[slot]).wait()

    def unit_b(unit):
        slot = unit % RING_B
        if unit < TAP9:
            src = h_ma.at[unit]
        else:
            local = unit - TAP9
            order = (3, 4, 5, 0, 1, 2, 6, 7, SUB)[local // 2]
            src = h_mb.at[order, pl.ds((local % 2) * C2, C2)]
        return pltpu.make_async_copy(src, ring_b.at[slot], sem_b.at[slot])

    def wait_b(unit):
        slot = unit % RING_B
        pltpu.make_async_copy(h_ma.at[0], ring_b.at[slot], sem_b.at[slot]).wait()

    cp_e1b.start()
    cp_e2a.start()
    for unit in range(TAP9):
        unit_a(unit).start()
    for unit in range(RING_B):
        unit_b(unit).start()
    for unit in range(TAP9, RING_A):
        unit_a(unit).start()

    barrier = pltpu.get_barrier_semaphore()
    for strip in range(1, STRIPS):
        other = (me + strip) % STRIPS
        other_col, other_row = owner(other)
        pl.semaphore_signal(barrier, inc=1, device_id=device(other_col, other_row), device_id_type=MESH_ID)
    pl.semaphore_wait(barrier, LAST)

    def is_me(strip_col, strip_row):
        return AND(strip_col == col, strip_row == row)

    def remote(src, dst, send, recv, strip_col, strip_row):
        return pltpu.make_async_remote_copy(src_ref=src, dst_ref=dst, send_sem=send, recv_sem=recv,
                                            device_id=device(strip_col, strip_row), device_id_type=MESH_ID)

    for k in range(SIDE):
        to_col, to_row = owner(4 * row + k)
        here = is_me(to_col, to_row)
        copy = remote(x_ref.at[pl.ds(SUB * k, STRIPS)], xb.at[col], x_send.at[k], x_recv.at[col], to_col, to_row)

        @pl.when(NOT(here))
        def _():
            copy.start()

        @pl.when(here)
        def _():
            xb[pl.ds(col, 1)] = x_ref[SUB * k:SUB * k + STRIPS][None]

    def halo_target(strip):
        return owner(jnp.clip(strip, 0, LAST))

    for side, (strip, allowed, first) in enumerate(((4 * row - 1, row > 0, 0), (4 * row + 4, row < 3, W3))):
        to_col, to_row = halo_target(strip)
        here = is_me(to_col, to_row)
        copy = remote(x_ref.at[pl.ds(first, SUB)], xh.at[col], h_send.at[side], h_recv.at[col], to_col, to_row)

        @pl.when(AND(allowed, NOT(here)))
        def _():
            copy.start()

        @pl.when(AND(allowed, here))
        def _():
            xh[pl.ds(col, 1)] = x_ref[first:first + SUB][None]

    for c in range(SIDE):
        @pl.when(NOT(is_me(c, row) & (row == col)))
        def _():
            remote(x_ref.at[pl.ds(0, STRIPS)], xb.at[c], x_send.at[0], x_recv.at[c], col, row).wait_recv()

    has_top = AND(k_me == 0, col > 0)
    has_bottom = AND(k_me == 3, col < 3)
    halo_row = jnp.where(has_top, col - 1, col + 1)
    for c in range(SIDE):
        own = AND(c == col, row == halo_row)

        @pl.when(AND(OR(has_top, has_bottom), NOT(own)))
        def _():
            remote(x_ref.at[pl.ds(0, SUB)], xh.at[c], h_send.at[0], h_recv.at[c], col, row).wait_recv()

    for k in range(SIDE):
        to_col, to_row = owner(4 * row + k)

        @pl.when(NOT(is_me(to_col, to_row)))
        def _():
            remote(x_ref.at[pl.ds(SUB * k, STRIPS)], xb.at[col], x_send.at[k], x_recv.at[col], to_col, to_row).wait_send()

    for side, (strip, allowed, first) in enumerate(((4 * row - 1, row > 0, 0), (4 * row + 4, row < 3, W3))):
        to_col, to_row = halo_target(strip)

        @pl.when(AND(allowed, NOT(is_me(to_col, to_row))))
        def _():
            remote(x_ref.at[pl.ds(first, SUB)], xh.at[col], h_send.at[side], h_recv.at[col], to_col, to_row).wait_send()

    lanes16 = lax.broadcasted_iota(jnp.int32, (STRIPS, LANE), 1)
    rows16 = lax.broadcasted_iota(jnp.int32, (STRIPS, LANE), 0)
    planes = [jnp.zeros((STRIPS, LANE), F32) for _ in range(SIDE)]
    for c in range(SIDE):
        halo = xh[c]
        both = jnp.concatenate([halo, halo], axis=0)
        top_rows = AND(has_top, rows16 < 2)
        bottom_rows = AND(has_bottom, AND(rows16 >= 10, rows16 < 12))
        block = jnp.where(OR(top_rows, bottom_rows), both, xb[c])
        inside = AND(lanes16 >= W3 * c, lanes16 < W3 * c + W3)
        for channel in range(SIDE):
            shift = (W3 * c - W3 * channel) % LANE
            moved = block if shift == 0 else pltpu.roll(block, shift, 1)
            planes[channel] = jnp.where(inside, moved, planes[channel])
    z[...] = jnp.zeros_like(z)
    for dx in TAPS:
        for channel in range(SIDE):
            plane = planes[channel]
            if dx == 0:
                plane = jnp.where(lanes16 == 0, 0.0, pltpu.roll(plane, 1, 1))
            elif dx == 2:
                plane = jnp.where(lanes16 == 127, 0.0, pltpu.roll(plane, 127, 1))
            z[pl.ds(dx * 4 + channel, STRIPS, stride=STRIPS), :] = plane

    def first_conv(j, carry):
        start = pl.multiple_of(j * STRIPS, STRIPS)
        taps = z[pl.ds(start, 48), :].astype(BF16)
        value = lax.dot_general(taps, w_e1a[...], (((0,), (0,)), ((), ())), preferred_element_type=F32)
        value = relu(value + bias[:1, :C1P])
        outside = OR(AND(me == 0, j == 0), AND(me == LAST, j == 9))
        value = jnp.where(outside, 0.0, value)
        act1[pl.ds(pl.multiple_of(j * LANE, LANE), LANE), :] = value.astype(BF16)
        return carry

    lax.fori_loop(0, 10, first_conv, 0)

    up_col, up_row = owner(jnp.maximum(me - 1, 0))
    down_col, down_row = owner(jnp.minimum(me + 1, LAST))

    def halo_copies(ref, width, height, index):
        to_up = remote(ref.at[pl.ds(width, width)], ref.at[pl.ds((height + 1) * width, width)],
                       e_send.at[index, 0], e_recv.at[index, 0], up_col, up_row)
        to_down = remote(ref.at[pl.ds(height * width, width)], ref.at[pl.ds(0, width)],
                         e_send.at[index, 1], e_recv.at[index, 1], down_col, down_row)
        return to_up, to_down

    def halo_start(ref, width, height, index):
        to_up, to_down = halo_copies(ref, width, height, index)

        @pl.when(me > 0)
        def _():
            to_up.start()

        @pl.when(me < LAST)
        def _():
            to_down.start()

        @pl.when(me == 0)
        def _():
            ref[:width, :] = jnp.zeros((width, ref.shape[1]), BF16)

        @pl.when(me == LAST)
        def _():
            ref[(height + 1) * width:(height + 2) * width, :] = jnp.zeros((width, ref.shape[1]), BF16)

    def halo_wait(ref, width, height, index):
        to_up, to_down = halo_copies(ref, width, height, index)

        @pl.when(me > 0)
        def _():
            to_down.wait_recv()
            to_up.wait_send()

        @pl.when(me < LAST)
        def _():
            to_up.wait_recv()
            to_down.wait_send()

    def build_tail(weights, base, tail):
        def body(dy, carry):
            parts = [weights[dy * 3 + dx, base:base + C1, TILE:C1].astype(F32) for dx in TAPS]
            zero = jnp.zeros((C1, HALF), F32)
            pair = jnp.concatenate([parts[0], parts[1]], axis=1)
            last = jnp.concatenate([parts[2], zero], axis=1)
            tail[dy, :, :LANE] = pair.astype(BF16)
            tail[dy, :, LANE:TILE] = last.astype(BF16)
            return carry

        lax.fori_loop(0, 3, body, 0)

    def narrow_lhs(ref, start, rows, width):
        mains = [ref[pl.ds(start + dy * width, rows), :TILE] for dy in TAPS]
        tails = [ref[pl.ds(start + dy * width, rows), TILE:C1P] for dy in TAPS]
        pair = (tails[0].astype(F32) + pltpu.roll(tails[1].astype(F32), HALF, 1)).astype(BF16)
        return jnp.concatenate(mains + [pair, tails[2][:, :HALF]], axis=1)

    def narrow_rhs(load):
        return jnp.concatenate([load(dy, 0, TILE) for dy in TAPS] + [load(dy, TILE, C1) for dy in TAPS], axis=0)

    x_index = column_index(TILE, LANE)
    not_first = x_index > 0
    not_last = x_index < 127

    def conv_level1(blocks, bias_row, finish):
        def chunk(i, carry):
            start = pl.multiple_of(i * TILE, TILE)
            lefts = [narrow_lhs(ref, start, TILE, LANE) for ref, _, _, _ in blocks]
            for dx in TAPS:
                pm[dx, SUB:END, :] = sum_of(
                    dot(left, narrow_rhs(lambda dy, a, b: weights[dy * 3 + dx, base + a:base + b, :TILE]))
                    for left, (_, weights, base, _) in zip(lefts, blocks))
            pt[SUB:END, :] = sum_of(dot(left, narrow_rhs(lambda dy, a, b: tail[dy, a:b, :]))
                                    for left, (_, _, _, tail) in zip(lefts, blocks))
            pieces = []
            for block in range(2):
                lanes = slice(block * LANE, block * LANE + LANE)
                value = pm[1, SUB:END, lanes] + jnp.where(not_first, pm[0, 7:263, lanes], 0.0)
                value = value + jnp.where(not_last, pm[2, 9:265, lanes], 0.0)
                pieces.append(relu(value + bias[bias_row:bias_row + 1, lanes]))
            value = pltpu.roll(pt[SUB:END, :LANE], HALF, 1) + jnp.where(not_first, pt[7:263, :LANE], 0.0)
            value = value + jnp.where(not_last, pt[9:265, LANE:TILE], 0.0)
            value = relu(value + bias[bias_row:bias_row + 1, TILE:C1P])
            pieces.append(jnp.where(lane_mask((TILE, LANE), HALF), value, 0.0))
            finish(i, pieces)
            return carry

        lax.fori_loop(0, 4, chunk, 0)

    def store_level1(ref):
        def finish(i, pieces):
            start = pl.multiple_of(LANE + i * TILE, LANE)
            for block in range(3):
                ref[pl.ds(start, TILE), block * LANE:block * LANE + LANE] = pieces[block].astype(BF16)
        return finish

    def finish_s1(i, pieces):
        store_level1(s1)(i, pieces)
        start = pl.multiple_of(HALF + i * HALF, HALF)
        for block in range(3):
            pool[:LANE, :] = jnp.maximum(pieces[block][:LANE], pieces[block][LANE:TILE])
            pooled = jnp.maximum(pool[pl.ds(0, HALF, stride=2), :], pool[pl.ds(1, HALF, stride=2), :])
            p1[pl.ds(start, HALF), block * LANE:block * LANE + LANE] = pooled.astype(BF16)

    cp_e1b.wait()
    build_tail(v_e1b, 0, t_e1b)
    conv_level1([(act1, v_e1b, 0, t_e1b)], 1, finish_s1)
    halo_start(p1, HALF, 4, 0)
    halo_start(s1, LANE, SUB, 1)

    x_index2 = column_index(TILE, HALF)
    not_first2 = x_index2 > 0
    not_last2 = x_index2 < 63

    def finish_level2(bias_row, store):
        def body(block, carry):
            lanes = pl.ds(pl.multiple_of(block * LANE, LANE), LANE)
            value = pl2[1, SUB:END, lanes] + jnp.where(not_first2, pl2[0, 7:263, lanes], 0.0)
            value = value + jnp.where(not_last2, pl2[2, 9:265, lanes], 0.0)
            store(lanes, relu(value + bias[bias_row:bias_row + 1, lanes]))
            return carry

        lax.fori_loop(0, 5, body, 0)

    def store_level2(ref, start):
        def store(lanes, value):
            ref[start:start + TILE, lanes] = value.astype(BF16)
        return store

    def store_s2(lanes, value):
        s2[HALF:C1, lanes] = value.astype(BF16)
        for i in range(2):
            pool[:HALF, :] = jnp.maximum(value[LANE * i:LANE * i + HALF], value[LANE * i + HALF:LANE * i + LANE])
            pooled = jnp.maximum(pool[pl.ds(0, W3, stride=2), :], pool[pl.ds(1, W3, stride=2), :])
            p2[W3 + W3 * i:HALF + W3 * i, lanes] = pooled.astype(BF16)

    NTILES = ((0, TILE), (TILE, 512), (512, C2))

    def stack_rows(ref, rows, width):
        return jnp.concatenate([ref[dy * width:dy * width + rows, :] for dy in TAPS], axis=1)

    halo_wait(p1, HALF, 4, 0)
    cp_e2a.wait()

    def enc2a(dx, carry):
        left = narrow_lhs(p1, 0, TILE, HALF)
        for a, b in NTILES:
            right = narrow_rhs(lambda dy, r0, r1: v_e2a[dy * 3 + dx, r0:r1, a:b])
            pl2[dx, SUB:END, a:b] = dot(left, right)
        return carry

    lax.fori_loop(0, 3, enc2a, 0)
    finish_level2(2, store_level2(act2, HALF))
    halo_start(act2, HALF, 4, 2)

    for unit in range(TAP9):
        wait_a(unit)
    halo_wait(act2, HALF, 4, 2)

    def conv640(ref, slots):
        def body(dx, carry):
            left = stack_rows(ref, TILE, HALF)
            picks = slots(dx)
            for a, b in NTILES:
                right = jnp.concatenate([ring_a[pick, :, a:b] for pick in picks], axis=0)
                pl2[dx, SUB:END, a:b] = dot(left, right)
            return carry

        lax.fori_loop(0, 3, body, 0)

    conv640(act2, lambda dx: [dy * 3 + dx for dy in TAPS])
    finish_level2(3, store_s2)
    halo_start(p2, W3, 2, 3)
    halo_start(s2, HALF, 4, 4)
    for unit in range(RING_A, A_REFILL):
        unit_a(unit).start()

    x_index3 = column_index(HALF, W3)
    not_first3 = x_index3 > 0
    not_last3 = x_index3 < 31

    def finish_level3(bias_row, ref, start):
        def body(block, carry):
            lanes = pl.ds(pl.multiple_of(block * LANE, LANE), LANE)
            value = pl3[1, SUB:72, lanes] + jnp.where(not_first3, pl3[0, 7:71, lanes], 0.0)
            value = value + jnp.where(not_last3, pl3[2, 9:73, lanes], 0.0)
            ref[start:start + HALF, lanes] = relu(value + bias[bias_row:bias_row + 1, lanes]).astype(BF16)
            return carry

        lax.fori_loop(0, 10, body, 0)

    for unit in range(TAP9):
        wait_b(unit)
    halo_wait(p2, W3, 2, 3)

    def mid_a(dx, carry):
        left = stack_rows(p2, HALF, W3)
        for n in range(5):
            right = jnp.concatenate([ring_b[dy * 3 + dx, :, n * TILE:n * TILE + TILE] for dy in TAPS], axis=0)
            pl3[dx, SUB:72, n * TILE:n * TILE + TILE] = dot(left, right)
        return carry

    lax.fori_loop(0, 3, mid_a, 0)
    finish_level3(4, act3, W3)
    halo_start(act3, W3, 2, 5)
    for unit in range(RING_B, RING_B + TAP9):
        unit_b(unit).start()
    cp_up1.start()
    cp_d1a.start()
    cp_d1b.start()
    halo_wait(act3, W3, 2, 5)

    def mid_b_tap(tap):
        dy = (1, 0, 2)[tap // 3]
        dx = tap % 3
        first = 9 + 2 * tap
        wait_b(first)
        wait_b(first + 1)
        left = act3[dy * W3:dy * W3 + HALF, :]

        def body(n, carry):
            lanes = pl.ds(pl.multiple_of(n * TILE, TILE), TILE)
            right = jnp.concatenate([ring_b[(first + half) % RING_B, :, lanes] for half in range(2)], axis=0)
            part = dot(left, right)
            if tap < 3:
                pl3[dx, SUB:72, lanes] = part
            else:
                pl3[dx, SUB:72, lanes] = pl3[dx, SUB:72, lanes] + part
            return carry

        lax.fori_loop(0, 5, body, 0)
        for unit in (first + RING_B, first + 1 + RING_B):
            if RING_B + TAP9 <= unit < B_END:
                unit_b(unit).start()

    for tap in range(TAP9):
        mid_b_tap(tap)
    finish_level3(5, mid, 0)

    for unit in range(TAP9, A_D2A):
        wait_a(unit)
    for tap in range(SIDE):
        p, q = tap // 2, tap % 2
        left = mid[...]
        for a, b in NTILES:
            right = jnp.concatenate([ring_a[(9 + 2 * tap + half) % RING_A, :, a:b] for half in range(2)], axis=0)
            part = dot(left, right)
            for i in range(2):
                for c0 in range(a, b, LANE):
                    up_f32[pl.ds(c0 * 2 + (2 * i + p) * HALF + q, W3, stride=2), :] = part[W3 * i:W3 * i + W3, c0 - a:c0 - a + LANE]
    for block in range(5):
        u2[HALF:C1, block * LANE:block * LANE + LANE] = up_f32[block * TILE:block * TILE + TILE, :].astype(BF16)
    halo_start(u2, HALF, 4, 6)
    for unit in range(A_REFILL, A_D2B):
        unit_a(unit).start()
    halo_wait(s2, HALF, 4, 4)
    halo_wait(u2, HALF, 4, 6)
    for unit in range(A_D2A, A_D2B):
        wait_a(unit)

    def dec2a(dx, carry):
        lefts = [stack_rows(u2, TILE, HALF), stack_rows(s2, TILE, HALF)]
        for a, b in NTILES:
            pl2[dx, SUB:END, a:b] = sum_of(
                dot(left, jnp.concatenate([ring_a[lax.rem(A_D2A + dx * 6 + dy * 2 + half, RING_A), :, a:b] for dy in TAPS], axis=0))
                for half, left in enumerate(lefts))
        return carry

    lax.fori_loop(0, 3, dec2a, 0)
    for unit in range(A_D2B, A_END):
        unit_a(unit).start()
    finish_level2(6, store_level2(act4, HALF))
    halo_start(act4, HALF, 4, 7)
    for unit in range(A_D2B, A_END):
        wait_a(unit)
    halo_wait(act4, HALF, 4, 7)
    conv640(act4, lambda dx: [lax.rem(A_D2B + dx * 3 + dy, RING_A) for dy in TAPS])
    finish_level2(7, store_level2(d2, 0))

    cp_up1.wait()
    for tap in range(SIDE):
        p, q = tap // 2, tap % 2
        left = d2[...]
        for a, b in ((0, TILE), (TILE, C1)):
            part = dot(left, v_up1[tap, :, a:b])
            for i in range(SIDE):
                for c0 in range(a, b, LANE):
                    c1 = min(b, c0 + LANE)
                    up_f32[pl.ds(c0 * SUB + (2 * i + p) * LANE + q, HALF, stride=2), :c1 - c0] = part[HALF * i:HALF * i + HALF, c0 - a:c1 - a]
    for block in range(3):
        value = up_f32[block * 1024:block * 1024 + 1024, :]
        if block == 2:
            value = jnp.where(lane_mask((1024, LANE), HALF), value, 0.0)
        u1[LANE:1152, block * LANE:block * LANE + LANE] = value.astype(BF16)
    halo_start(u1, LANE, SUB, SUB)
    cp_d1a.wait()
    build_tail(v_d1a, 0, t_d1a.at[0])
    build_tail(v_d1a, C1, t_d1a.at[1])
    halo_wait(s1, LANE, SUB, 1)
    halo_wait(u1, LANE, SUB, SUB)
    conv_level1([(u1, v_d1a, 0, t_d1a.at[0]), (s1, v_d1a, C1, t_d1a.at[1])], SUB, store_level1(act5))
    halo_start(act5, LANE, SUB, 9)
    cp_d1b.wait()
    build_tail(v_d1b, 0, t_d1b)
    halo_wait(act5, LANE, SUB, 9)

    def finish_head(i, pieces):
        value = jnp.concatenate([piece.astype(BF16) for piece in pieces], axis=1)
        head = lax.dot_general(w_head[...], value, (((1,), (1,)), ((), ())), preferred_element_type=F32)
        ys[pl.ds(i, 1)] = head[None]

    conv_level1([(act5, v_d1b, 0, t_d1b)], 9, finish_head)

    lanes8 = lax.broadcasted_iota(jnp.int32, (SUB, LANE), 1)
    sub8 = lax.broadcasted_iota(jnp.int32, (SUB, LANE), 0)
    for c in range(SIDE):
        packed = jnp.zeros((SUB, LANE), F32)
        for y in range(SUB):
            line = ys[y // 2, :, (y % 2) * LANE:(y % 2) * LANE + LANE]
            slot = y % 4
            shift = (W3 * slot - W3 * c) % LANE
            line = line if shift == 0 else pltpu.roll(line, shift, 1)
            if y >= 4:
                line = pltpu.roll(line, 4, 0)
            place = AND(AND(lanes8 >= W3 * slot, lanes8 < W3 * slot + W3), (sub8 >= 4) if y >= 4 else (sub8 < 4))
            packed = jnp.where(place, line, packed)
        ysend[c] = packed

    def y_copy(c):
        return remote(ysend.at[c], yrecv.at[k_me], y_send.at[c], y_recv.at[k_me], c, col)

    for c in range(SIDE):
        here = is_me(c, col)

        @pl.when(NOT(here))
        def _():
            y_copy(c).start()

        @pl.when(here)
        def _():
            yrecv[pl.ds(k_me, 1)] = ysend[c][None]

    for k in range(SIDE):
        from_col, from_row = owner(4 * row + k)

        @pl.when(NOT(is_me(from_col, from_row)))
        def _():
            remote(ysend.at[0], yrecv.at[k], y_send.at[0], y_recv.at[k], col, row).wait_recv()

    for c in range(SIDE):
        @pl.when(NOT(is_me(c, col)))
        def _():
            y_copy(c).wait_send()

    out_ref[...] = yrecv[...]


def network(x, w_e1a, bias, w_head, *weights):
    vmem = pl.BlockSpec(memory_space=pltpu.VMEM)
    hbm = pl.BlockSpec(memory_space=pl.ANY)
    dma = pltpu.SemaphoreType.DMA
    scratch = [
        pltpu.VMEM((4, STRIPS, LANE), F32), pltpu.VMEM((4, SUB, LANE), F32), pltpu.VMEM((TILE, LANE), F32),
        pltpu.VMEM((C3, C1P), BF16), pltpu.VMEM((C3, C1P), BF16), pltpu.VMEM((C1P, C1P), BF16),
        pltpu.VMEM((C1P, C2), BF16), pltpu.VMEM((C1P, C2), BF16), pltpu.VMEM((LANE, C2), BF16),
        pltpu.VMEM((LANE, C3), BF16), pltpu.VMEM((HALF, C3), BF16), pltpu.VMEM((C1P, C2), BF16),
        pltpu.VMEM((C1P, C2), BF16), pltpu.VMEM((TILE, C2), BF16), pltpu.VMEM((C3, C1P), BF16), pltpu.VMEM((C3, C1P), BF16),
        pltpu.VMEM((9, C1, C1), BF16), pltpu.VMEM((9, C2, C1), BF16), pltpu.VMEM((9, C1, C1), BF16),
        pltpu.VMEM((4, C2, C1), BF16), pltpu.VMEM((9, C1, C2), BF16),
        pltpu.VMEM((3, C1, TILE), BF16), pltpu.VMEM((2, 3, C1, TILE), BF16), pltpu.VMEM((3, C1, TILE), BF16),
        pltpu.VMEM((RING_A, C2, C2), BF16), pltpu.VMEM((RING_B, C2, C3), BF16),
        pltpu.VMEM((3, MARGIN, TILE), F32), pltpu.VMEM((MARGIN, TILE), F32), pltpu.VMEM((3, MARGIN, C2), F32), pltpu.VMEM((3, 80, C3), F32),
        pltpu.VMEM((LANE, LANE), F32), pltpu.VMEM((3072, LANE), F32), pltpu.VMEM((4, SUB, TILE), F32),
        pltpu.VMEM((4, SUB, LANE), F32), pltpu.VMEM((4, SUB, LANE), F32),
        dma((5,)), dma((RING_A,)), dma((RING_B,)), dma((4,)), dma((4,)), dma((2,)), dma((4,)),
        dma((10, 2)), dma((10, 2)), dma((4,)), dma((4,)),
    ]
    return pl.pallas_call(
        kernel,
        out_shape=jax.ShapeDtypeStruct((4, SUB, LANE), F32),
        in_specs=[vmem] * 4 + [hbm] * 11,
        out_specs=vmem,
        scratch_shapes=scratch,
        compiler_params=pltpu.CompilerParams(collective_id=0, has_side_effects=True, vmem_limit_bytes=66 * 1000 * 1000),
        name="unet",
    )(x, w_e1a, bias, w_head, *weights)


def solution(mesh):
    tile_spec = P(("data", "row"), "col", None)

    def device_body(tile, *params):
        (w_enc1a, b_enc1a, w_enc1b, b_enc1b, w_enc2a, b_enc2a, w_enc2b, b_enc2b,
         w_mid_a, b_mid_a, w_mid_b, b_mid_b, w_up2, w_dec2a, b_dec2a, w_dec2b, b_dec2b,
         w_up1, w_dec1a, b_dec1a, w_dec1b, b_dec1b, w_head, b_head) = params
        x = jnp.transpose(tile, (0, 2, 1)).reshape(W3, LANE).astype(F32)
        x = jnp.pad(x, ((2, 6), (0, 0)))
        first = jnp.pad(w_enc1a.reshape(3, 12, C1), ((0, 0), (0, 4), (0, HALF))).reshape(48, C1P)
        biases = (b_enc1a, b_enc1b, b_enc2a, b_enc2b, b_mid_a, b_mid_b, b_dec2a, b_dec2b, b_dec1a, b_dec1b)
        bias = jnp.stack([jnp.pad(b, (0, C3 - b.shape[0])) for b in biases])
        head = jnp.pad(w_head.T, ((0, 4), (0, HALF)))

        def taps(weight):
            return weight.reshape(-1, weight.shape[2], weight.shape[3])

        weights = [taps(w) for w in (w_enc1b, w_enc2a, w_enc2b, w_mid_a, w_mid_b, w_up2, w_dec2a, w_dec2b, w_up1, w_dec1a, w_dec1b)]
        packed = network(x, first, bias, head, *weights)
        out = packed.reshape(4, 2, 4, 4, W3).transpose(0, 1, 3, 4, 2).reshape(W3, W3, 4)
        return out + b_head

    def program(image, *params):
        mapped = jax.shard_map(device_body, mesh=mesh, in_specs=(tile_spec,) + tuple([P()] * len(params)), out_specs=tile_spec, check_vma=False)
        return mapped(image, *params)

    return program
```

profile of v0, /device:TPU:1, one launch (start us, length us, event | category | flops | bytes accessed | tf_op | source)
XLA Modules:
  0.0 111.1 jit_solution(13174210082320133557)
XLA Ops:
  0.0 0.7 stack.37
  0.7 0.7 stack.38
  1.4 1.3 %pad.51.w_head = bf16[8,384]{1,0:T(8,128)(2,1)} pad(bf16[4,320]{1,0:T(4,128)(2,1)} %bitcast.31, bf16[]{:T(256)} %constant.4.clone.1), padding=0_4x0_64 | pad | bytes 8706 | tf_op jit(solution)/shard_map/jit(_pad)/pad | solution.py:640
  2.7 0.8 convert_element_type.24
  3.5 0.7 pad.43
  4.2 0.7 pad.44
  4.9 0.7 pad.45
  5.6 0.7 pad.46
  6.3 0.7 pad.47
  7.0 0.7 pad.48
  7.7 0.7 pad.49
  8.4 0.7 pad.50
  9.1 0.6 pad_convert_fusion.x_ref
  9.7 1.3 %stack.43.bias = f32[10,1280]{1,0:T(8,128)} concatenate(f32[1,1280]{1,0:T(1,128)S(1)} %stack.33, f32[1,1280]{1,0:T(1,128)S(1)} %stack.34, f32[1,1280]{1,0:T(1,128)S(1)} %stack.35, f32[1,1280]{1,0:T(1,128)S(1)} %stack.36, f32[1,1280]{1,0:T(1,128)S(1)} %stack.37, f32[1,1280]{1,0:T(1,128)S(1)} %stack.38, f32[1,1280]{1,0:T(1,128)S(1)} %stack.39, f32[1,1280]{1,0:T(1,128)S(1)} %stack.40, ...), dimensions={0} | concatenate | bytes 102400 | tf_op jit(solution)/shard_map/stack | solution.py:639
  11.0 0.8 reshape.49
  11.8 0.6 pad.42
  12.4 3.7 %copy.26 = bf16[2,2,640,320]{3,2,1,0:T(8,128)(2,1)} copy(bf16[2,2,640,320]{2,3,1,0:T(8,128)(2,1)} %param.43) | data formatting | bytes 3276800 | tf_op args[18]
  16.1 7.7 %copy.27 = bf16[3,3,640,320]{3,2,1,0:T(8,128)(2,1)} copy(bf16[3,3,640,320]{2,3,1,0:T(8,128)(2,1)} %param.44) | data formatting | bytes 7372800 | tf_op args[19]
  23.8 0.0 copy-start
  23.8 85.7 %unet.1 = f32[4,8,128]{2,1,0:T(8,128)} custom-call(f32[40,128]{1,0:T(8,128)} %pad_convert_fusion.x_ref, bf16[48,384]{1,0:T(8,128)(2,1)} %bitcast.29, f32[10,1280]{1,0:T(8,128)} %stack.43.bias, bf16[8,384]{1,0:T(8,128)(2,1)} %pad.51.w_head, bf16[9,320,320]{2,1,0:T(8,128)(2,1)} %bitcast.26, bf16[9,320,640]{2,1,0:T(8,128)(2,1)} %bitcast.25, ...), custom_call_target="tpu_custom_call" | custom-call | tf_op jit(solution)/shard_map/unet/pallas_call | solution.py:617
  109.5 0.8 reshape.62
  110.4 0.0 copy-done
  110.4 0.7 bitcast_add_fusion
  (9 shorter events, 0.1 us)
Async XLA Ops:
  23.8 86.5 %copy-start = (f32[4]{0:T(128)S(1)}, f32[4]{0:T(128)}, u32[]{:S(2)}) copy-start(f32[4]{0:T(128)} %param.49) | copy-start | bytes 52
where the time goes:
time: 112 us; the launch traced here: 111 us
  Pallas kernels  85.7 us (77%)
  local copies, waits for them, and re-layouts  24 us (21%)
  other arithmetic  1.31 us (1%)
    pallas_call x1, Pallas kernels, network(): pl.pallas_call(kernel, out_shape=jax.ShapeDtypeStruct((4, SUB, LANE), F32...  85.7 us
    unnamed x4, local copies, waits for them, and re-layouts  11.4 us
    pad x8, local copies, waits for them, and re-layouts, device_body(): bias = jnp.stack([jnp.pad(b, (0, C3 - b.shape[0])) for b in biases])  5.5 us
    another operation x11, local copies, waits for them, and re-layouts, device_body(): bias = jnp.stack([jnp.pad(b, (0, C3 - b.shape[0])) for b in biases])  2.78 us

commit v1 on v0

v1 whole, which is shorter than its diff:
```python
import jax
import jax.numpy as jnp
from jax import lax
from jax.experimental import pallas as pl
from jax.experimental.pallas import tpu as pltpu
from jax.sharding import PartitionSpec as P

F32 = jnp.float32
BF16 = jnp.bfloat16
STRIPS = 16
LAST = STRIPS - 1
SIDE = 4
SUB, LANE = 8, 128
TILE, HALF = 2 * LANE, LANE // 2
C1, C2, C3, C1P = 320, 640, 1280, 384
W3 = 32
END = SUB + TILE
MARGIN = END + SUB
TAPS = range(3)
TAP9 = 9
RING = 50
E2B, MA, MB, UP2, D2A, D2B, UP1, D1A, UNITS = 0, 9, 27, 63, 71, 89, 98, 100, 105
ROWS = (1, 0, 2)
NOT = jnp.logical_not
AND = jnp.logical_and
OR = jnp.logical_or
MESH_ID = pl.DeviceIdType.MESH


def dot(lhs, rhs):
    return jnp.dot(lhs, rhs, preferred_element_type=F32)


def sum_of(parts):
    first, *rest = parts
    for part in rest:
        first = first + part
    return first


def relu(value):
    return jnp.maximum(value, 0.0)


def lane_mask(shape, below):
    return lax.broadcasted_iota(jnp.int32, shape, 1) < below


def column_index(rows, width):
    return lax.rem(lax.broadcasted_iota(jnp.int32, (rows, LANE), 0), width)


def kernel(x_ref, w_e1a, w_head, *refs):
    biases, refs = refs[:10], refs[10:]
    (h_e1b, h_e2a, h_e2b, h_ma, h_mb, h_up2, h_d2a, h_d2b, h_up1, h_d1a, h_d1b,
     out_ref,
     xb, xh, z, act1, cat1, p1, act2, s2, p2, act3, mid, u2, act4, d2, act5,
     v_e1b, v_e2a, t_e1b, ring, bias, w_first, w_out,
     pm, pt, pl2, pl3, pd1, pool, up_f32, ys, ysend, yrecv,
     sem_w, sem_r, x_send, x_recv, h_send, h_recv, e_send, e_recv, y_send, y_recv) = refs
    col = lax.axis_index("col")
    row = lax.axis_index("row")
    data = lax.axis_index("data")

    def owner(strip):
        strip_col = strip // 4
        k = strip % 4
        return strip_col, k + (strip_col % 2) * (3 - 2 * k)

    def device(strip_col, strip_row):
        return (data, strip_col, strip_row)

    k_me = row + (col % 2) * (3 - 2 * row)
    me = 4 * col + k_me

    def whole(src, dst, index):
        return pltpu.make_async_copy(src, dst, sem_w.at[index])

    cp_e1b = whole(h_e1b, v_e1b, 0)
    cp_e2a = whole(h_e2a, v_e2a, 1)
    cp_d1b = whole(h_d1b, v_e1b, 2)

    def half(index):
        return pl.ds((index % 2) * C2, C2)

    def unit(index):
        slot = index % RING
        dst = ring.at[slot]
        if index < MA:
            src = h_e2b.at[index]
        elif index < MB:
            tap = (index - MA) // 2
            src = h_ma.at[ROWS[tap // 3] * 3 + tap % 3, :, half(index - MA)]
        elif index < UP2:
            local = index - MB
            tap = local // 4
            src = h_mb.at[ROWS[tap // 3] * 3 + tap % 3, half(local // 2), half(local)]
        elif index < D2A:
            local = index - UP2
            src = h_up2.at[local // 2, half(local)]
        elif index < D2B:
            local = (index - D2A) % TAP9
            src = h_d2a.at[(local % 3) * 3 + local // 3, half((D2B - 1 - index) // TAP9)]
        elif index < UP1:
            local = index - D2B
            src = h_d2b.at[(local % 3) * 3 + local // 3]
        elif index < D1A:
            src = h_up1.at[pl.ds((index - UP1) * C2, C2)]
        elif index < UNITS - 1:
            src = h_d1a.at[pl.ds((index - D1A) * C2, C2)]
        else:
            src = h_d1a.at[pl.ds((index - D1A) * C2, C1)]
            dst = ring.at[slot, pl.ds(0, C1)]
        return pltpu.make_async_copy(src, dst, sem_r.at[slot])

    def wait_units(first, last):
        for index in range(first, last):
            unit(index).wait()

    def refill(done):
        for index in range(done[0] + RING, min(done[1] + RING, UNITS)):
            unit(index).start()

    cp_e1b.start()
    cp_e2a.start()
    for index in range(RING):
        unit(index).start()

    bias[...] = jnp.zeros_like(bias)
    for index, ref in enumerate(biases):
        bias[index:index + 1, :ref.shape[0]] = ref[...].reshape(1, ref.shape[0])
    w_first[...] = jnp.zeros_like(w_first)
    for tap in range(TAP9):
        at = (tap // 3) * STRIPS + (tap % 3) * SIDE
        w_first[at:at + SIDE, :C1] = w_e1a[tap].astype(F32)
    w_out[...] = jnp.zeros_like(w_out)
    w_out[:SIDE, :C1] = w_head[...].astype(F32)

    barrier = pltpu.get_barrier_semaphore()
    for strip in range(1, STRIPS):
        other = (me + strip) % STRIPS
        other_col, other_row = owner(other)
        pl.semaphore_signal(barrier, inc=1, device_id=device(other_col, other_row), device_id_type=MESH_ID)
    pl.semaphore_wait(barrier, LAST)

    def is_me(strip_col, strip_row):
        return AND(strip_col == col, strip_row == row)

    def remote(src, dst, send, recv, strip_col, strip_row):
        return pltpu.make_async_remote_copy(src_ref=src, dst_ref=dst, send_sem=send, recv_sem=recv,
                                            device_id=device(strip_col, strip_row), device_id_type=MESH_ID)

    for k in range(SIDE):
        to_col, to_row = owner(4 * row + k)
        here = is_me(to_col, to_row)
        copy = remote(x_ref.at[pl.ds(SUB * k, STRIPS)], xb.at[col], x_send.at[k], x_recv.at[col], to_col, to_row)

        @pl.when(NOT(here))
        def _():
            copy.start()

        @pl.when(here)
        def _():
            xb[pl.ds(col, 1)] = x_ref[SUB * k:SUB * k + STRIPS][None]

    def halo_target(strip):
        return owner(jnp.clip(strip, 0, LAST))

    for side, (strip, allowed, first) in enumerate(((4 * row - 1, row > 0, 0), (4 * row + 4, row < 3, W3))):
        to_col, to_row = halo_target(strip)
        here = is_me(to_col, to_row)
        copy = remote(x_ref.at[pl.ds(first, SUB)], xh.at[col], h_send.at[side], h_recv.at[col], to_col, to_row)

        @pl.when(AND(allowed, NOT(here)))
        def _():
            copy.start()

        @pl.when(AND(allowed, here))
        def _():
            xh[pl.ds(col, 1)] = x_ref[first:first + SUB][None]

    for c in range(SIDE):
        @pl.when(NOT(is_me(c, row) & (row == col)))
        def _():
            remote(x_ref.at[pl.ds(0, STRIPS)], xb.at[c], x_send.at[0], x_recv.at[c], col, row).wait_recv()

    has_top = AND(k_me == 0, col > 0)
    has_bottom = AND(k_me == 3, col < 3)
    halo_row = jnp.where(has_top, col - 1, col + 1)
    for c in range(SIDE):
        own = AND(c == col, row == halo_row)

        @pl.when(AND(OR(has_top, has_bottom), NOT(own)))
        def _():
            remote(x_ref.at[pl.ds(0, SUB)], xh.at[c], h_send.at[0], h_recv.at[c], col, row).wait_recv()

    for k in range(SIDE):
        to_col, to_row = owner(4 * row + k)

        @pl.when(NOT(is_me(to_col, to_row)))
        def _():
            remote(x_ref.at[pl.ds(SUB * k, STRIPS)], xb.at[col], x_send.at[k], x_recv.at[col], to_col, to_row).wait_send()

    for side, (strip, allowed, first) in enumerate(((4 * row - 1, row > 0, 0), (4 * row + 4, row < 3, W3))):
        to_col, to_row = halo_target(strip)

        @pl.when(AND(allowed, NOT(is_me(to_col, to_row))))
        def _():
            remote(x_ref.at[pl.ds(first, SUB)], xh.at[col], h_send.at[side], h_recv.at[col], to_col, to_row).wait_send()

    lanes16 = lax.broadcasted_iota(jnp.int32, (STRIPS, LANE), 1)
    rows16 = lax.broadcasted_iota(jnp.int32, (STRIPS, LANE), 0)
    planes = [jnp.zeros((STRIPS, LANE), F32) for _ in range(SIDE)]
    for c in range(SIDE):
        halo = xh[c]
        both = jnp.concatenate([halo, halo], axis=0)
        top_rows = AND(has_top, rows16 < 2)
        bottom_rows = AND(has_bottom, AND(rows16 >= 10, rows16 < 12))
        block = jnp.where(OR(top_rows, bottom_rows), both, xb[c])
        inside = AND(lanes16 >= W3 * c, lanes16 < W3 * c + W3)
        for channel in range(SIDE):
            shift = (W3 * c - W3 * channel) % LANE
            moved = block if shift == 0 else pltpu.roll(block, shift, 1)
            planes[channel] = jnp.where(inside, moved, planes[channel])
    z[...] = jnp.zeros_like(z)
    for dx in TAPS:
        for channel in range(SIDE):
            plane = planes[channel]
            if dx == 0:
                plane = jnp.where(lanes16 == 0, 0.0, pltpu.roll(plane, 1, 1))
            elif dx == 2:
                plane = jnp.where(lanes16 == 127, 0.0, pltpu.roll(plane, 127, 1))
            z[pl.ds(dx * 4 + channel, STRIPS, stride=STRIPS), :] = plane

    def first_conv(pair, carry):
        weights = w_first[...].astype(BF16)
        for j in (2 * pair, 2 * pair + 1):
            taps = z[pl.ds(pl.multiple_of(j * STRIPS, STRIPS), 48), :].astype(BF16)
            value = lax.dot_general(taps, weights, (((0,), (0,)), ((), ())), preferred_element_type=F32)
            value = relu(value + bias[:1, :C1P])
            outside = OR(AND(me == 0, j == 0), AND(me == LAST, j == TAP9))
            value = jnp.where(outside, 0.0, value)
            act1[pl.ds(pl.multiple_of(j * LANE, LANE), LANE), :] = value.astype(BF16)
        return carry

    lax.fori_loop(0, 5, first_conv, 0)

    up_col, up_row = owner(jnp.maximum(me - 1, 0))
    down_col, down_row = owner(jnp.minimum(me + 1, LAST))

    def clear_borders(ref, width, height):
        @pl.when(me == 0)
        def _():
            ref[:width, :] = jnp.zeros((width, ref.shape[1]), BF16)

        @pl.when(me == LAST)
        def _():
            ref[(height + 1) * width:(height + 2) * width, :] = jnp.zeros((width, ref.shape[1]), BF16)

    for ref, width, height in ((cat1, LANE, SUB), (act5, LANE, SUB), (p1, HALF, SIDE), (act2, HALF, SIDE), (s2, HALF, SIDE),
                               (u2, HALF, SIDE), (act4, HALF, SIDE), (p2, W3, 2), (act3, W3, 2)):
        clear_borders(ref, width, height)

    def halo_copies(ref, width, height, index, lanes):
        to_up = remote(ref.at[pl.ds(width, width), lanes], ref.at[pl.ds((height + 1) * width, width), lanes],
                       e_send.at[index, 0], e_recv.at[index, 0], up_col, up_row)
        to_down = remote(ref.at[pl.ds(height * width, width), lanes], ref.at[pl.ds(0, width), lanes],
                         e_send.at[index, 1], e_recv.at[index, 1], down_col, down_row)
        return to_up, to_down

    def halo_start(ref, width, height, index, lanes=slice(None)):
        to_up, to_down = halo_copies(ref, width, height, index, lanes)

        @pl.when(me > 0)
        def _():
            to_up.start()

        @pl.when(me < LAST)
        def _():
            to_down.start()

    def halo_wait(ref, width, height, index, lanes=slice(None)):
        to_up, to_down = halo_copies(ref, width, height, index, lanes)

        @pl.when(me > 0)
        def _():
            to_down.wait_recv()
            to_up.wait_send()

        @pl.when(me < LAST)
        def _():
            to_up.wait_recv()
            to_down.wait_send()

    def build_tail(weights, base, tail):
        def body(dy, carry):
            parts = [weights[dy * 3 + dx, base:base + C1, TILE:C1].astype(F32) for dx in TAPS]
            zero = jnp.zeros((C1, HALF), F32)
            pair = jnp.concatenate([parts[0], parts[1]], axis=1)
            last = jnp.concatenate([parts[2], zero], axis=1)
            tail[dy, :, :LANE] = pair.astype(BF16)
            tail[dy, :, LANE:TILE] = last.astype(BF16)
            return carry

        lax.fori_loop(0, 3, body, 0)

    def narrow_lhs(ref, start, rows, width):
        mains = [ref[pl.ds(start + dy * width, rows), :TILE] for dy in TAPS]
        tails = [ref[pl.ds(start + dy * width, rows), TILE:C1P] for dy in TAPS]
        pair = (tails[0].astype(F32) + pltpu.roll(tails[1].astype(F32), HALF, 1)).astype(BF16)
        return jnp.concatenate(mains + [pair, tails[2][:, :HALF]], axis=1)

    def narrow_rhs(load):
        return jnp.concatenate([load(dy, 0, TILE) for dy in TAPS] + [load(dy, TILE, C1) for dy in TAPS], axis=0)

    x_index = column_index(TILE, LANE)
    not_first = x_index > 0
    not_last = x_index < 127

    low_half = lane_mask((TILE, LANE), HALF)

    def shifted(ref, plane, left, right):
        first = left + jnp.where(not_first, ref[plane(0) + (slice(7, 263), right[0])], 0.0)
        return first + jnp.where(not_last, ref[plane(2) + (slice(9, 265), right[1])], 0.0)

    def blocks_of(block):
        return slice(block * LANE, block * LANE + LANE)

    def conv_narrow(ref, bias_row, finish, chunks):
        def chunk(step, carry):
            i = chunks[0] + step * chunks[1]
            start = pl.multiple_of(i * TILE, TILE)
            left = narrow_lhs(ref, start, TILE, LANE)
            for dx in TAPS:
                pm[dx, SUB:END, :] = dot(left, narrow_rhs(lambda dy, a, b: v_e1b[dy * 3 + dx, a:b, :TILE]))
            pt[SUB:END, :] = dot(left, narrow_rhs(lambda dy, a, b: t_e1b[dy, a:b, :]))
            pieces = []
            for block in range(2):
                lanes = blocks_of(block)
                value = shifted(pm, lambda dx: (dx,), pm[1, SUB:END, lanes], (lanes, lanes))
                pieces.append(relu(value + bias[bias_row:bias_row + 1, lanes]))
            value = shifted(pt, lambda dx: (), pltpu.roll(pt[SUB:END, :LANE], HALF, 1), (blocks_of(0), blocks_of(1)))
            value = relu(value + bias[bias_row:bias_row + 1, TILE:C1P])
            pieces.append(jnp.where(low_half, value, 0.0))
            finish(i, pieces)
            return carry

        lax.fori_loop(0, 2, chunk, 0)

    def conv_cat(bias_row, finish, chunks):
        def chunk(step, carry):
            i = chunks[0] + step * chunks[1]
            start = pl.multiple_of(i * TILE, TILE)
            left = jnp.concatenate([cat1[pl.ds(start + dy * LANE, TILE), :] for dy in TAPS], axis=1)
            right = jnp.concatenate([jnp.concatenate([d1a_tap(dy * 3 + dx) for dx in TAPS], axis=0) for dy in TAPS], axis=1)
            pd1[SUB:END, :960] = lax.dot_general(left, right, (((1,), (1,)), ((), ())), preferred_element_type=F32)
            turned = [pltpu.roll(pd1[SUB:END, blocks_of(2 + block)], HALF, 1) for block in TAPS]
            pieces = []
            for block in TAPS:
                middle = turned[block] if block == 2 else jnp.where(low_half, turned[block], turned[block + 1])
                value = shifted(pd1, lambda dx: (), middle, (blocks_of(block), blocks_of(5 + block) if block < 2 else slice(896, 1024)))
                value = relu(value + bias[bias_row:bias_row + 1, blocks_of(block)])
                pieces.append(value if block < 2 else jnp.where(low_half, value, 0.0))
            finish(i, pieces)
            return carry

        lax.fori_loop(0, 2, chunk, 0)

    def store_level1(ref):
        def finish(i, pieces):
            start = pl.multiple_of(LANE + i * TILE, LANE)
            for block in range(3):
                ref[pl.ds(start, TILE), block * LANE:block * LANE + LANE] = pieces[block].astype(BF16)
        return finish

    def finish_s1(i, pieces):
        at = pl.ds(pl.multiple_of(LANE + i * TILE, LANE), TILE)
        turned = [pltpu.roll(piece, HALF, 1) for piece in pieces]
        cat1[at, TILE:C1P] = jnp.where(low_half, 0.0, turned[0]).astype(BF16)
        for block in range(2):
            cat1[at, blocks_of(3 + block)] = jnp.where(low_half, turned[block], turned[block + 1]).astype(BF16)
        start = pl.multiple_of(HALF + i * HALF, HALF)
        for block in range(3):
            pool[:LANE, :] = jnp.maximum(pieces[block][:LANE], pieces[block][LANE:TILE])
            pooled = jnp.maximum(pool[pl.ds(0, HALF, stride=2), :], pool[pl.ds(1, HALF, stride=2), :])
            p1[pl.ds(start, HALF), block * LANE:block * LANE + LANE] = pooled.astype(BF16)

    S1_LANES = pl.ds(C1P, TILE)
    U1_LANES = pl.ds(0, C1P)
    cp_e1b.wait()
    build_tail(v_e1b, 0, t_e1b)
    conv_narrow(act1, 1, finish_s1, (0, 3))
    halo_start(p1, HALF, SIDE, 0)
    halo_start(cat1, LANE, SUB, 1, S1_LANES)
    conv_narrow(act1, 1, finish_s1, (1, 1))
    cp_d1b.start()

    x_index2 = column_index(TILE, HALF)
    not_first2 = x_index2 > 0
    not_last2 = x_index2 < 63

    def finish_level2(bias_row, store):
        def body(block, carry):
            lanes = pl.ds(pl.multiple_of(block * LANE, LANE), LANE)
            value = pl2[1, SUB:END, lanes] + jnp.where(not_first2, pl2[0, 7:263, lanes], 0.0)
            value = value + jnp.where(not_last2, pl2[2, 9:265, lanes], 0.0)
            store(lanes, relu(value + bias[bias_row:bias_row + 1, lanes]))
            return carry

        lax.fori_loop(0, 5, body, 0)

    def store_level2(ref, start):
        def store(lanes, value):
            ref[start:start + TILE, lanes] = value.astype(BF16)
        return store

    def store_s2(lanes, value):
        s2[HALF:C1, lanes] = value.astype(BF16)
        for i in range(2):
            pool[:HALF, :] = jnp.maximum(value[LANE * i:LANE * i + HALF], value[LANE * i + HALF:LANE * i + LANE])
            pooled = jnp.maximum(pool[pl.ds(0, W3, stride=2), :], pool[pl.ds(1, W3, stride=2), :])
            p2[W3 + W3 * i:HALF + W3 * i, lanes] = pooled.astype(BF16)

    NTILES = ((0, TILE), (TILE, 512), (512, C2))

    def stack_rows(ref, rows, width):
        return jnp.concatenate([ref[dy * width:dy * width + rows, :] for dy in TAPS], axis=1)

    halo_wait(p1, HALF, 4, 0)
    cp_e2a.wait()

    def enc2a(dx, carry):
        left = narrow_lhs(p1, 0, TILE, HALF)
        for a, b in NTILES:
            right = narrow_rhs(lambda dy, r0, r1: v_e2a[dy * 3 + dx, r0:r1, a:b])
            pl2[dx, SUB:END, a:b] = dot(left, right)
        return carry

    lax.fori_loop(0, 3, enc2a, 0)
    finish_level2(2, store_level2(act2, HALF))
    halo_start(act2, HALF, 4, 2)

    wait_units(E2B, MA)
    halo_wait(act2, HALF, 4, 2)

    def conv640(ref, slots):
        def body(dx, carry):
            left = stack_rows(ref, TILE, HALF)
            picks = slots(dx)
            for a, b in NTILES:
                right = jnp.concatenate([ring[pick, :, a:b] for pick in picks], axis=0)
                pl2[dx, SUB:END, a:b] = dot(left, right)
            return carry

        lax.fori_loop(0, 3, body, 0)

    conv640(act2, lambda dx: [dy * 3 + dx for dy in TAPS])
    finish_level2(3, store_s2)
    halo_start(p2, W3, 2, 3)
    halo_start(s2, HALF, 4, 4)
    refill((E2B, MA))

    x_index3 = column_index(HALF, W3)
    not_first3 = x_index3 > 0
    not_last3 = x_index3 < 31

    def finish_level3(bias_row, ref, start):
        def body(block, carry):
            lanes = pl.ds(pl.multiple_of(block * LANE, LANE), LANE)
            value = pl3[1, SUB:72, lanes] + jnp.where(not_first3, pl3[0, 7:71, lanes], 0.0)
            value = value + jnp.where(not_last3, pl3[2, 9:73, lanes], 0.0)
            ref[start:start + HALF, lanes] = relu(value + bias[bias_row:bias_row + 1, lanes]).astype(BF16)
            return carry

        lax.fori_loop(0, 10, body, 0)

    def slot_of(index):
        return lax.rem(index, RING)

    def wide(first):
        return jnp.concatenate([ring[slot_of(first)], ring[slot_of(first + 1)]], axis=1)

    def add_rows(dx, value):
        pl3[dx, SUB:72, :] = pl3[dx, SUB:72, :] + value

    def mid_a_own(dx, carry):
        pl3[dx, SUB:72, :] = dot(p2[W3:3 * W3, :], wide(MA + 2 * dx))
        return carry

    def mid_a_halo(dx, carry):
        left = jnp.concatenate([p2[:HALF, :], p2[HALF:LANE, :]], axis=1)
        add_rows(dx, dot(left, jnp.concatenate([wide(MA + 6 + 2 * dx), wide(MA + 12 + 2 * dx)], axis=0)))
        return carry

    wait_units(MA, MB)
    lax.fori_loop(0, 3, mid_a_own, 0)
    halo_wait(p2, W3, 2, 3)
    lax.fori_loop(0, 3, mid_a_halo, 0)
    finish_level3(4, act3, W3)
    halo_start(act3, W3, 2, 5)
    refill((MA, MB))

    for group, dy in enumerate(ROWS):
        def mid_b(dx, carry):
            first = MB + (group * 3 + dx) * SIDE
            for part in range(SIDE):
                slot = slot_of(first + part)
                pltpu.make_async_copy(h_e2b.at[0], ring.at[slot], sem_r.at[slot]).wait()
            value = dot(act3[dy * W3:dy * W3 + HALF, :], jnp.concatenate([wide(first), wide(first + 2)], axis=0))
            if group:
                add_rows(dx, value)
            else:
                pl3[dx, SUB:72, :] = value
            return carry

        if group == 1:
            halo_wait(act3, W3, 2, 5)
        lax.fori_loop(0, 3, mid_b, 0)
        refill((MB + group * 12, MB + group * 12 + 12))
    finish_level3(5, mid, 0)

    wait_units(UP2, D2A)
    for tap in range(SIDE):
        p, q = tap // 2, tap % 2
        left = mid[...]
        for a, b in NTILES:
            right = jnp.concatenate([ring[(UP2 + 2 * tap + part) % RING, :, a:b] for part in range(2)], axis=0)
            part = dot(left, right)
            for i in range(2):
                for c0 in range(a, b, LANE):
                    up_f32[pl.ds(c0 * 2 + (2 * i + p) * HALF + q, W3, stride=2), :] = part[W3 * i:W3 * i + W3, c0 - a:c0 - a + LANE]
    for block in range(5):
        u2[HALF:C1, block * LANE:block * LANE + LANE] = up_f32[block * TILE:block * TILE + TILE, :].astype(BF16)
    halo_start(u2, HALF, 4, 6)
    refill((UP2, D2A))
    halo_wait(s2, HALF, SIDE, 4)

    def dec2a(ref, first, dx):
        left = stack_rows(ref, TILE, HALF)
        for a, b in NTILES:
            right = jnp.concatenate([ring[slot_of(first + dx * 3 + dy), :, a:b] for dy in TAPS], axis=0)
            yield a, b, dot(left, right)

    def dec2a_skip(dx, carry):
        for a, b, value in dec2a(s2, D2A, dx):
            pl2[dx, SUB:END, a:b] = value
        return carry

    def dec2a_up(dx, carry):
        for a, b, value in dec2a(u2, D2A + TAP9, dx):
            pl2[dx, SUB:END, a:b] = pl2[dx, SUB:END, a:b] + value
        return carry

    wait_units(D2A, D2A + TAP9)
    lax.fori_loop(0, 3, dec2a_skip, 0)
    refill((D2A, D2A + TAP9))
    wait_units(D2A + TAP9, D2B)
    halo_wait(u2, HALF, SIDE, 6)
    lax.fori_loop(0, 3, dec2a_up, 0)
    refill((D2A + TAP9, D2B))
    finish_level2(6, store_level2(act4, HALF))
    halo_start(act4, HALF, 4, 7)
    wait_units(D2B, UP1)
    halo_wait(act4, HALF, 4, 7)
    conv640(act4, lambda dx: [slot_of(D2B + dx * 3 + dy) for dy in TAPS])
    finish_level2(7, store_level2(d2, 0))

    def half1(tap):
        return slice((tap % 2) * C1, (tap % 2) * C1 + C1)

    refill((D2B, UP1))
    wait_units(UP1, D1A)
    for tap in range(SIDE):
        p, q = tap // 2, tap % 2
        left = d2[...]
        up = lax.dot_general(left, ring[(UP1 + tap // 2) % RING, half1(tap), :], (((1,), (1,)), ((), ())), preferred_element_type=F32)
        for a, b in ((0, TILE), (TILE, C1)):
            part = up[:, a:b]
            for i in range(SIDE):
                for c0 in range(a, b, LANE):
                    c1 = min(b, c0 + LANE)
                    up_f32[pl.ds(c0 * SUB + (2 * i + p) * LANE + q, HALF, stride=2), :c1 - c0] = part[HALF * i:HALF * i + HALF, c0 - a:c1 - a]
    for block in TAPS:
        value = up_f32[block * 1024:block * 1024 + 1024, :].astype(BF16)
        if block < 2:
            cat1[LANE:TILE + 7 * LANE, blocks_of(block)] = value
        else:
            cat1[LANE:TILE + 7 * LANE, TILE:C1] = value[:, :HALF]
    halo_start(cat1, LANE, SUB, 8, U1_LANES)

    def d1a_tap(tap):
        return ring[(D1A + tap // 2) % RING, half1(tap), :]

    wait_units(D1A, UNITS)
    conv_cat(8, store_level1(act5), (1, 1))
    halo_wait(cat1, LANE, SUB, 1, S1_LANES)
    halo_wait(cat1, LANE, SUB, 8, U1_LANES)
    conv_cat(8, store_level1(act5), (0, 3))
    halo_start(act5, LANE, SUB, 9)
    cp_d1b.wait()
    build_tail(v_e1b, 0, t_e1b)

    def finish_head(i, pieces):
        value = jnp.concatenate([piece.astype(BF16) for piece in pieces], axis=1)
        head = lax.dot_general(w_out[...].astype(BF16), value, (((1,), (1,)), ((), ())), preferred_element_type=F32)
        ys[pl.ds(i, 1)] = head[None]

    conv_narrow(act5, TAP9, finish_head, (1, 1))
    halo_wait(act5, LANE, SUB, 9)
    conv_narrow(act5, TAP9, finish_head, (0, 3))

    lanes8 = lax.broadcasted_iota(jnp.int32, (SUB, LANE), 1)
    sub8 = lax.broadcasted_iota(jnp.int32, (SUB, LANE), 0)
    for c in range(SIDE):
        packed = jnp.zeros((SUB, LANE), F32)
        for y in range(SUB):
            line = ys[y // 2, :, (y % 2) * LANE:(y % 2) * LANE + LANE]
            slot = y % 4
            shift = (W3 * slot - W3 * c) % LANE
            line = line if shift == 0 else pltpu.roll(line, shift, 1)
            if y >= 4:
                line = pltpu.roll(line, 4, 0)
            place = AND(AND(lanes8 >= W3 * slot, lanes8 < W3 * slot + W3), (sub8 >= 4) if y >= 4 else (sub8 < 4))
            packed = jnp.where(place, line, packed)
        ysend[c] = packed

    def y_copy(c):
        return remote(ysend.at[c], yrecv.at[k_me], y_send.at[c], y_recv.at[k_me], c, col)

    for c in range(SIDE):
        here = is_me(c, col)

        @pl.when(NOT(here))
        def _():
            y_copy(c).start()

        @pl.when(here)
        def _():
            yrecv[pl.ds(k_me, 1)] = ysend[c][None]

    for k in range(SIDE):
        from_col, from_row = owner(4 * row + k)

        @pl.when(NOT(is_me(from_col, from_row)))
        def _():
            remote(ysend.at[0], yrecv.at[k], y_send.at[0], y_recv.at[k], col, row).wait_recv()

    for c in range(SIDE):
        @pl.when(NOT(is_me(c, col)))
        def _():
            y_copy(c).wait_send()

    out_ref[...] = yrecv[...]


def network(x, w_e1a, w_head, *rest):
    vmem = pl.BlockSpec(memory_space=pltpu.VMEM)
    hbm = pl.BlockSpec(memory_space=pl.ANY)
    dma = pltpu.SemaphoreType.DMA
    scratch = [pltpu.VMEM(shape, F32) for shape in ((SIDE, STRIPS, LANE), (SIDE, SUB, LANE), (TILE, LANE))]
    level1, level2 = 10 * LANE, 6 * HALF
    scratch += [pltpu.VMEM(shape, BF16) for shape in (
        (level1, C1P), (level1, C2), (level2, C1P), (level2, C2), (level2, C2), (LANE, C2), (LANE, C3), (HALF, C3),
        (level2, C2), (level2, C2), (TILE, C2), (level1, C1P),
        (TAP9, C1, C1), (TAP9, C1, C2), (3, C1, TILE), (RING, C2, C2))]
    scratch += [pltpu.VMEM(shape, F32) for shape in (
        (10, C3), (48, C1P), (SUB, C1P),
        (3, MARGIN, TILE), (MARGIN, TILE), (3, MARGIN, C2), (3, 80, C3), (MARGIN, 1024),
        (LANE, LANE), (3072, LANE), (SIDE, SUB, TILE), (SIDE, SUB, LANE), (SIDE, SUB, LANE))]
    scratch += [dma(shape) for shape in ((3,), (RING,), (SIDE,), (SIDE,), (2,), (SIDE,), (10, 2), (10, 2), (SIDE,), (SIDE,))]
    return pl.pallas_call(
        kernel,
        out_shape=jax.ShapeDtypeStruct((SIDE, SUB, LANE), F32),
        in_specs=[vmem] * 13 + [hbm] * 11,
        out_specs=vmem,
        scratch_shapes=scratch,
        compiler_params=pltpu.CompilerParams(collective_id=0, has_side_effects=True, vmem_limit_bytes=67043328),
        name="unet",
    )(x, w_e1a, w_head, *rest)


def solution(mesh):
    tile_spec = P(("data", "row"), "col", None)

    def device_body(tile, *params):
        (w_enc1a, b_enc1a, w_enc1b, b_enc1b, w_enc2a, b_enc2a, w_enc2b, b_enc2b,
         w_mid_a, b_mid_a, w_mid_b, b_mid_b, w_up2, w_dec2a, b_dec2a, w_dec2b, b_dec2b,
         w_up1, w_dec1a, b_dec1a, w_dec1b, b_dec1b, w_head, b_head) = params
        x = jnp.transpose(tile, (0, 2, 1)).reshape(W3, LANE).astype(F32)
        x = jnp.pad(x, ((2, 6), (0, 0)))
        biases = (b_enc1a, b_enc1b, b_enc2a, b_enc2b, b_mid_a, b_mid_b, b_dec2a, b_dec2b, b_dec1a, b_dec1b)

        def taps(weight):
            return weight.reshape(-1, weight.shape[2], weight.shape[3])

        def turned(weight):
            return jnp.swapaxes(weight, 2, 3).reshape(-1, weight.shape[2])

        weights = [taps(w) for w in (w_enc1b, w_enc2a, w_enc2b, w_mid_a, w_mid_b, w_up2, w_dec2a, w_dec2b)]
        weights += [turned(w_up1), turned(w_dec1a), taps(w_dec1b)]
        packed = network(x, taps(w_enc1a), w_head.T, *biases, *weights)
        out = packed.reshape(4, 2, 4, 4, W3).transpose(0, 1, 3, 4, 2).reshape(W3, W3, 4)
        return out + b_head

    def program(image, *params):
        mapped = jax.shard_map(device_body, mesh=mesh, in_specs=(tile_spec,) + tuple([P()] * len(params)), out_specs=tile_spec, check_vma=False)
        return mapped(image, *params)

    return program
```

time: 112 us -> 77.8 us (0.69)
  local copies, waits for them, and re-layouts: 24 us -> 1.67 us
  Pallas kernels: 85.7 us -> 73.8 us
    pallas_call x1, Pallas kernels: 85.7 us -> 73.8 us  [network(): pl.pallas_call(kernel, out_shape=jax.ShapeDtypeStruct((SIDE, SUB, LANE),...]
    unnamed x4 -> x0, local copies, waits for them, and re-layouts: 11.4 us -> none
    pad x10 -> x0, local copies, waits for them, and re-layouts: 7.41 us -> none  [the longest x8 5.5 us: device_body(): bias = jnp.stack([jnp.pad(b, (0, C3 - b.shape[0])) for b in biases])]
    another operation x11 -> x0, local copies, waits for them, and re-layouts: 2.78 us -> none  [device_body(): bias = jnp.stack([jnp.pad(b, (0, C3 - b.shape[0])) for b in biases])]
where the time goes in v1:
time: 77.8 us; the launch traced here: 77.5 us
  Pallas kernels  73.8 us (95%)
  other arithmetic  1.98 us (3%)
  local copies, waits for them, and re-layouts  1.67 us (2%)
    pallas_call x1, Pallas kernels, network(): pl.pallas_call(kernel, out_shape=jax.ShapeDtypeStruct((SIDE, SUB, LANE),...  73.8 us

profile of v1, /device:TPU:1, one launch (start us, length us, event | category | flops | bytes accessed | tf_op | source)
XLA Modules:
  0.0 77.5 jit_solution(16627393545170031228)
XLA Ops:
  0.0 0.8 %convert_element_type.10 = bf16[32,128]{1,0:T(8,128)(2,1)S(1)} reshape(bf16[32,4,32]{2,1,0:T(4,128)(2,1)} %bitcast.33) | data formatting | bytes 16384 | tf_op jit(solution)/shard_map/convert_element_type | solution.py:689
  0.9 0.6 pad_convert_fusion.x_ref
  1.5 73.8 %unet.1 = f32[4,8,128]{2,1,0:T(8,128)} custom-call(f32[40,128]{1,0:T(8,128)} %pad_convert_fusion.x_ref, bf16[9,4,320]{2,1,0:T(4,128)(2,1)} %bitcast.34, bf16[4,320]{1,0:T(4,128)(2,1)} %bitcast.35, f32[320]{0:T(512)} %refs_0_.1, f32[320]{0:T(512)} %refs_1_.1, f32[640]{0:T(1024)} %refs_2_.1, f32[640]{0:T(1024)} %refs_3_.1, f32[1280]{0:T(1024)} %refs_4_.1, ...), custom_call_target="tpu_custom_call" | custom-call | tf_op jit(solution)/shard_map/unet/pallas_call | solution.py:671
  75.3 0.8 %reshape.58 = f32[4,2,4,4,32]{4,3,2,1,0:T(4,128)S(1)} reshape(f32[4,8,128]{2,1,0:T(8,128)} %unet.1) | data formatting | bytes 32768 | tf_op jit(solution)/shard_map/reshape | solution.py:702
  76.1 1.4 %bitcast_add_fusion = f32[32,32,4]{1,2,0:T(4,128)} fusion(f32[4,2,4,32,4]{3,4,2,1,0:T(4,128)S(1)} %copy.26, f32[4]{0:T(128)} %param.49), kind=kLoop, calls=%fused_computation | loop fusion | flops 4096 | bytes 32784 | tf_op jit(solution)/shard_map/add | solution.py:703
  (1 shorter events, 0.0 us)

commit v2 on v1

--- a/solution.py
+++ b/solution.py
@@ -17,6 +17,8 @@
 END = SUB + TILE
 MARGIN = END + SUB
 TAPS = range(3)
+PAIR = range(2)
+QUAD = range(SIDE)
 TAP9 = 9
 RING = 50
 E2B, MA, MB, UP2, D2A, D2B, UP1, D1A, UNITS = 0, 9, 27, 63, 71, 89, 98, 100, 105
@@ -31,15 +33,24 @@
     return jnp.dot(lhs, rhs, preferred_element_type=F32)
 
 
-def sum_of(parts):
-    first, *rest = parts
-    for part in rest:
-        first = first + part
-    return first
-
-
 def relu(value):
     return jnp.maximum(value, 0.0)
+
+
+def dot_t(lhs, rhs):
+    return lax.dot_general(lhs, rhs, (((1,), (1,)), ((), ())), preferred_element_type=F32)
+
+
+def cat_lanes(parts):
+    return jnp.concatenate(list(parts), axis=1)
+
+
+def cat_rows(parts):
+    return jnp.concatenate(list(parts), axis=0)
+
+
+def turn(value, amount=HALF):
+    return value if amount == 0 else pltpu.roll(value, amount, 1)
 
 
 def lane_mask(shape, below):
@@ -54,7 +65,7 @@
     biases, refs = refs[:10], refs[10:]
     (h_e1b, h_e2a, h_e2b, h_ma, h_mb, h_up2, h_d2a, h_d2b, h_up1, h_d1a, h_d1b,
      out_ref,
-     xb, xh, z, act1, cat1, p1, act2, s2, p2, act3, mid, u2, act4, d2, act5,
+     xrows, xs, xb, xh, z, act1, cat1, p1, act2, s2, p2, act3, mid, u2, act4, d2, act5,
      v_e1b, v_e2a, t_e1b, ring, bias, w_first, w_out,
      pm, pt, pl2, pl3, pd1, pool, up_f32, ys, ysend, yrecv,
      sem_w, sem_r, x_send, x_recv, h_send, h_recv, e_send, e_recv, y_send, y_recv) = refs
@@ -73,6 +84,11 @@
     k_me = row + (col % 2) * (3 - 2 * row)
     me = 4 * col + k_me
 
+    barrier = pltpu.get_barrier_semaphore()
+    for strip in range(1, STRIPS):
+        other_col, other_row = owner((me + strip) % STRIPS)
+        pl.semaphore_signal(barrier, inc=1, device_id=device(other_col, other_row), device_id_type=MESH_ID)
+
     def whole(src, dst, index):
         return pltpu.make_async_copy(src, dst, sem_w.at[index])
 
@@ -87,7 +103,7 @@
         slot = index % RING
         dst = ring.at[slot]
         if index < MA:
-            src = h_e2b.at[index]
+            src = h_e2b.at[(index % 3) * 3 + index // 3]
         elif index < MB:
             tap = (index - MA) // 2
             src = h_ma.at[ROWS[tap // 3] * 3 + tap % 3, :, half(index - MA)]
@@ -136,11 +152,18 @@
     w_out[...] = jnp.zeros_like(w_out)
     w_out[:SIDE, :C1] = w_head[...].astype(F32)
 
-    barrier = pltpu.get_barrier_semaphore()
-    for strip in range(1, STRIPS):
-        other = (me + strip) % STRIPS
-        other_col, other_row = owner(other)
-        pl.semaphore_signal(barrier, inc=1, device_id=device(other_col, other_row), device_id_type=MESH_ID)
+    xrows[...] = jnp.zeros_like(xrows)
+    xrows[2:2 + W3, :SIDE, :W3] = x_ref[...].astype(F32)
+
+    def pack(group, carry):
+        packed = jnp.zeros((SUB, LANE), F32)
+        for j in range(SUB):
+            line = turn(xrows[group * SUB + j], (j % SIDE) * W3)
+            packed = packed + (line if j < SIDE else pltpu.roll(line, SIDE, 0))
+        xs[pl.ds(group, 1)] = packed[None]
+        return carry
+
+    lax.fori_loop(0, 5, pack, 0)
     pl.semaphore_wait(barrier, LAST)
 
     def is_me(strip_col, strip_row):
@@ -150,10 +173,10 @@
         return pltpu.make_async_remote_copy(src_ref=src, dst_ref=dst, send_sem=send, recv_sem=recv,
                                             device_id=device(strip_col, strip_row), device_id_type=MESH_ID)
 
-    for k in range(SIDE):
+    for k in QUAD:
         to_col, to_row = owner(4 * row + k)
         here = is_me(to_col, to_row)
-        copy = remote(x_ref.at[pl.ds(SUB * k, STRIPS)], xb.at[col], x_send.at[k], x_recv.at[col], to_col, to_row)
+        copy = remote(xs.at[pl.ds(k, 2)], xb.at[col], x_send.at[k], x_recv.at[col], to_col, to_row)
 
         @pl.when(NOT(here))
         def _():
@@ -161,15 +184,15 @@
 
         @pl.when(here)
         def _():
-            xb[pl.ds(col, 1)] = x_ref[SUB * k:SUB * k + STRIPS][None]
+            xb[pl.ds(col, 1)] = xs[k:k + 2][None]
 
     def halo_target(strip):
         return owner(jnp.clip(strip, 0, LAST))
 
-    for side, (strip, allowed, first) in enumerate(((4 * row - 1, row > 0, 0), (4 * row + 4, row < 3, W3))):
+    for side, (strip, allowed, first) in enumerate(((4 * row - 1, row > 0, 0), (4 * row + 4, row < 3, SIDE))):
         to_col, to_row = halo_target(strip)
         here = is_me(to_col, to_row)
-        copy = remote(x_ref.at[pl.ds(first, SUB)], xh.at[col], h_send.at[side], h_recv.at[col], to_col, to_row)
+        copy = remote(xs.at[pl.ds(first, 1)], xh.at[col], h_send.at[side], h_recv.at[col], to_col, to_row)
 
         @pl.when(AND(allowed, NOT(here)))
         def _():
@@ -177,60 +200,58 @@
 
         @pl.when(AND(allowed, here))
         def _():
-            xh[pl.ds(col, 1)] = x_ref[first:first + SUB][None]
-
-    for c in range(SIDE):
+            xh[pl.ds(col, 1)] = xs[first:first + 1][None]
+
+    for c in QUAD:
         @pl.when(NOT(is_me(c, row) & (row == col)))
         def _():
-            remote(x_ref.at[pl.ds(0, STRIPS)], xb.at[c], x_send.at[0], x_recv.at[c], col, row).wait_recv()
+            remote(xs.at[pl.ds(0, 2)], xb.at[c], x_send.at[0], x_recv.at[c], col, row).wait_recv()
 
     has_top = AND(k_me == 0, col > 0)
     has_bottom = AND(k_me == 3, col < 3)
     halo_row = jnp.where(has_top, col - 1, col + 1)
-    for c in range(SIDE):
+    for c in QUAD:
         own = AND(c == col, row == halo_row)
 
         @pl.when(AND(OR(has_top, has_bottom), NOT(own)))
         def _():
-            remote(x_ref.at[pl.ds(0, SUB)], xh.at[c], h_send.at[0], h_recv.at[c], col, row).wait_recv()
-
-    for k in range(SIDE):
+            remote(xs.at[pl.ds(0, 1)], xh.at[c], h_send.at[0], h_recv.at[c], col, row).wait_recv()
+
+    for k in QUAD:
         to_col, to_row = owner(4 * row + k)
 
         @pl.when(NOT(is_me(to_col, to_row)))
         def _():
-            remote(x_ref.at[pl.ds(SUB * k, STRIPS)], xb.at[col], x_send.at[k], x_recv.at[col], to_col, to_row).wait_send()
-
-    for side, (strip, allowed, first) in enumerate(((4 * row - 1, row > 0, 0), (4 * row + 4, row < 3, W3))):
+            remote(xs.at[pl.ds(k, 2)], xb.at[col], x_send.at[k], x_recv.at[col], to_col, to_row).wait_send()
+
+    for side, (strip, allowed, first) in enumerate(((4 * row - 1, row > 0, 0), (4 * row + 4, row < 3, SIDE))):
         to_col, to_row = halo_target(strip)
 
         @pl.when(AND(allowed, NOT(is_me(to_col, to_row))))
         def _():
-            remote(x_ref.at[pl.ds(first, SUB)], xh.at[col], h_send.at[side], h_recv.at[col], to_col, to_row).wait_send()
-
-    lanes16 = lax.broadcasted_iota(jnp.int32, (STRIPS, LANE), 1)
-    rows16 = lax.broadcasted_iota(jnp.int32, (STRIPS, LANE), 0)
-    planes = [jnp.zeros((STRIPS, LANE), F32) for _ in range(SIDE)]
-    for c in range(SIDE):
-        halo = xh[c]
-        both = jnp.concatenate([halo, halo], axis=0)
-        top_rows = AND(has_top, rows16 < 2)
-        bottom_rows = AND(has_bottom, AND(rows16 >= 10, rows16 < 12))
-        block = jnp.where(OR(top_rows, bottom_rows), both, xb[c])
-        inside = AND(lanes16 >= W3 * c, lanes16 < W3 * c + W3)
-        for channel in range(SIDE):
-            shift = (W3 * c - W3 * channel) % LANE
-            moved = block if shift == 0 else pltpu.roll(block, shift, 1)
-            planes[channel] = jnp.where(inside, moved, planes[channel])
+            remote(xs.at[pl.ds(first, 1)], xh.at[col], h_send.at[side], h_recv.at[col], to_col, to_row).wait_send()
+
+    lanes8 = lax.broadcasted_iota(jnp.int32, (SUB, LANE), 1)
+    sub8 = lax.broadcasted_iota(jnp.int32, (SUB, LANE), 0)
     z[...] = jnp.zeros_like(z)
-    for dx in TAPS:
-        for channel in range(SIDE):
-            plane = planes[channel]
-            if dx == 0:
-                plane = jnp.where(lanes16 == 0, 0.0, pltpu.roll(plane, 1, 1))
-            elif dx == 2:
-                plane = jnp.where(lanes16 == 127, 0.0, pltpu.roll(plane, 127, 1))
-            z[pl.ds(dx * 4 + channel, STRIPS, stride=STRIPS), :] = plane
+    halo_place = (AND(has_top, lanes8 < HALF), AND(has_bottom, lanes8 >= HALF))
+    for part in PAIR:
+        place = AND(halo_place[part], sub8 < SIDE)
+        blocks = [jnp.where(place, xh[c, 0], xb[c, part]) for c in QUAD]
+        for group in QUAD:
+            line = jnp.zeros((SUB, LANE), F32)
+            for c in QUAD:
+                inside = lanes8 // W3 == c
+                line = jnp.where(inside, turn(blocks[c], (W3 * (c - group)) % LANE), line)
+            for dx in TAPS:
+                moved = line
+                if dx == 0:
+                    moved = jnp.where(lanes8 == 0, 0.0, turn(line, 1))
+                elif dx == 2:
+                    moved = jnp.where(lanes8 == LANE - 1, 0.0, turn(line, LANE - 1))
+                for upper in range(2 - part):
+                    at = (part * SUB + group + upper * SIDE) * STRIPS + dx * SIDE
+                    z[at:at + SIDE, :] = moved[upper * SIDE:upper * SIDE + SIDE]
 
     def first_conv(pair, carry):
         weights = w_first[...].astype(BF16)
@@ -296,8 +317,8 @@
         def body(dy, carry):
             parts = [weights[dy * 3 + dx, base:base + C1, TILE:C1].astype(F32) for dx in TAPS]
             zero = jnp.zeros((C1, HALF), F32)
-            pair = jnp.concatenate([parts[0], parts[1]], axis=1)
-            last = jnp.concatenate([parts[2], zero], axis=1)
+            pair = cat_lanes(parts[:2])
+            last = cat_lanes([parts[2], zero])
             tail[dy, :, :LANE] = pair.astype(BF16)
             tail[dy, :, LANE:TILE] = last.astype(BF16)
             return carry
@@ -307,11 +328,11 @@
     def narrow_lhs(ref, start, rows, width):
         mains = [ref[pl.ds(start + dy * width, rows), :TILE] for dy in TAPS]
         tails = [ref[pl.ds(start + dy * width, rows), TILE:C1P] for dy in TAPS]
-        pair = (tails[0].astype(F32) + pltpu.roll(tails[1].astype(F32), HALF, 1)).astype(BF16)
-        return jnp.concatenate(mains + [pair, tails[2][:, :HALF]], axis=1)
+        pair = (tails[0].astype(F32) + turn(tails[1].astype(F32))).astype(BF16)
+        return cat_lanes(mains + [pair, tails[2][:, :HALF]])
 
     def narrow_rhs(load):
-        return jnp.concatenate([load(dy, 0, TILE) for dy in TAPS] + [load(dy, TILE, C1) for dy in TAPS], axis=0)
+        return cat_rows([load(dy, 0, TILE) for dy in TAPS] + [load(dy, TILE, C1) for dy in TAPS])
 
     x_index = column_index(TILE, LANE)
     not_first = x_index > 0
@@ -335,11 +356,11 @@
                 pm[dx, SUB:END, :] = dot(left, narrow_rhs(lambda dy, a, b: v_e1b[dy * 3 + dx, a:b, :TILE]))
             pt[SUB:END, :] = dot(left, narrow_rhs(lambda dy, a, b: t_e1b[dy, a:b, :]))
             pieces = []
-            for block in range(2):
+            for block in PAIR:
                 lanes = blocks_of(block)
                 value = shifted(pm, lambda dx: (dx,), pm[1, SUB:END, lanes], (lanes, lanes))
                 pieces.append(relu(value + bias[bias_row:bias_row + 1, lanes]))
-            value = shifted(pt, lambda dx: (), pltpu.roll(pt[SUB:END, :LANE], HALF, 1), (blocks_of(0), blocks_of(1)))
+            value = shifted(pt, lambda dx: (), turn(pt[SUB:END, :LANE]), (blocks_of(0), blocks_of(1)))
             value = relu(value + bias[bias_row:bias_row + 1, TILE:C1P])
             pieces.append(jnp.where(low_half, value, 0.0))
             finish(i, pieces)
@@ -351,10 +372,10 @@
         def chunk(step, carry):
             i = chunks[0] + step * chunks[1]
             start = pl.multiple_of(i * TILE, TILE)
-            left = jnp.concatenate([cat1[pl.ds(start + dy * LANE, TILE), :] for dy in TAPS], axis=1)
-            right = jnp.concatenate([jnp.concatenate([d1a_tap(dy * 3 + dx) for dx in TAPS], axis=0) for dy in TAPS], axis=1)
-            pd1[SUB:END, :960] = lax.dot_general(left, right, (((1,), (1,)), ((), ())), preferred_element_type=F32)
-            turned = [pltpu.roll(pd1[SUB:END, blocks_of(2 + block)], HALF, 1) for block in TAPS]
+            left = cat_lanes(cat1[pl.ds(start + dy * LANE, TILE), :] for dy in TAPS)
+            right = cat_lanes(cat_rows(d1a_tap(dy * 3 + dx) for dx in TAPS) for dy in TAPS)
+            pd1[SUB:END, :3 * C1] = dot_t(left, right)
+            turned = [turn(pd1[SUB:END, blocks_of(2 + block)]) for block in TAPS]
             pieces = []
             for block in TAPS:
                 middle = turned[block] if block == 2 else jnp.where(low_half, turned[block], turned[block + 1])
@@ -375,9 +396,9 @@
 
     def finish_s1(i, pieces):
         at = pl.ds(pl.multiple_of(LANE + i * TILE, LANE), TILE)
-        turned = [pltpu.roll(piece, HALF, 1) for piece in pieces]
+        turned = [turn(piece) for piece in pieces]
         cat1[at, TILE:C1P] = jnp.where(low_half, 0.0, turned[0]).astype(BF16)
-        for block in range(2):
+        for block in PAIR:
             cat1[at, blocks_of(3 + block)] = jnp.where(low_half, turned[block], turned[block + 1]).astype(BF16)
         start = pl.multiple_of(HALF + i * HALF, HALF)
         for block in range(3):
@@ -416,45 +437,48 @@
 
     def store_s2(lanes, value):
         s2[HALF:C1, lanes] = value.astype(BF16)
-        for i in range(2):
+        for i in PAIR:
             pool[:HALF, :] = jnp.maximum(value[LANE * i:LANE * i + HALF], value[LANE * i + HALF:LANE * i + LANE])
             pooled = jnp.maximum(pool[pl.ds(0, W3, stride=2), :], pool[pl.ds(1, W3, stride=2), :])
             p2[W3 + W3 * i:HALF + W3 * i, lanes] = pooled.astype(BF16)
 
-    NTILES = ((0, TILE), (TILE, 512), (512, C2))
-
-    def stack_rows(ref, rows, width):
-        return jnp.concatenate([ref[dy * width:dy * width + rows, :] for dy in TAPS], axis=1)
+    NTILES = ((0, TILE), (TILE, 2 * TILE), (2 * TILE, C2))
+    TAIL = slice(2 * TILE, C2)
+
+    def stack_rows(ref, rows, width, taps=TAPS):
+        return cat_lanes(ref[dy * width:dy * width + rows, :] for dy in taps)
+
+    def level2_taps(left, weights, add=False):
+        def put(dx, lanes, value):
+            pl2[dx, SUB:END, lanes] = pl2[dx, SUB:END, lanes] + value if add else value
+
+        for dx in TAPS:
+            for first, last in NTILES[:2]:
+                lanes = slice(first, last)
+                put(dx, lanes, dot(left, weights(dx, lanes)))
+        pair = dot(left, cat_lanes(weights(dx, TAIL) for dx in PAIR))
+        put(0, TAIL, pair[:, :LANE])
+        put(1, TAIL, pair[:, LANE:])
+        put(2, TAIL, dot(left, weights(2, TAIL)))
+
+    def unit_rows(first, taps=TAPS):
+        return lambda dx, lanes: cat_rows(ring[(first + dx * 3 + dy) % RING, :, lanes] for dy in taps)
 
     halo_wait(p1, HALF, 4, 0)
     cp_e2a.wait()
 
-    def enc2a(dx, carry):
-        left = narrow_lhs(p1, 0, TILE, HALF)
-        for a, b in NTILES:
-            right = narrow_rhs(lambda dy, r0, r1: v_e2a[dy * 3 + dx, r0:r1, a:b])
-            pl2[dx, SUB:END, a:b] = dot(left, right)
-        return carry
-
-    lax.fori_loop(0, 3, enc2a, 0)
+    level2_taps(narrow_lhs(p1, 0, TILE, HALF),
+                lambda dx, lanes: narrow_rhs(lambda dy, r0, r1: v_e2a[dy * 3 + dx, r0:r1, lanes]))
     finish_level2(2, store_level2(act2, HALF))
     halo_start(act2, HALF, 4, 2)
 
+    def conv640(ref, first, index):
+        level2_taps(ref[HALF:HALF + TILE, :], unit_rows(first, (1,)))
+        halo_wait(ref, HALF, SIDE, index)
+        level2_taps(stack_rows(ref, TILE, HALF, (0, 2)), unit_rows(first, (0, 2)), add=True)
+
     wait_units(E2B, MA)
-    halo_wait(act2, HALF, 4, 2)
-
-    def conv640(ref, slots):
-        def body(dx, carry):
-            left = stack_rows(ref, TILE, HALF)
-            picks = slots(dx)
-            for a, b in NTILES:
-                right = jnp.concatenate([ring[pick, :, a:b] for pick in picks], axis=0)
-                pl2[dx, SUB:END, a:b] = dot(left, right)
-            return carry
-
-        lax.fori_loop(0, 3, body, 0)
-
-    conv640(act2, lambda dx: [dy * 3 + dx for dy in TAPS])
+    conv640(act2, E2B, 2)
     finish_level2(3, store_s2)
     halo_start(p2, W3, 2, 3)
     halo_start(s2, HALF, 4, 4)
@@ -478,24 +502,18 @@
         return lax.rem(index, RING)
 
     def wide(first):
-        return jnp.concatenate([ring[slot_of(first)], ring[slot_of(first + 1)]], axis=1)
+        return cat_lanes([ring[slot_of(first)], ring[slot_of(first + 1)]])
 
     def add_rows(dx, value):
         pl3[dx, SUB:72, :] = pl3[dx, SUB:72, :] + value
 
-    def mid_a_own(dx, carry):
+    wait_units(MA, MB)
+    for dx in TAPS:
         pl3[dx, SUB:72, :] = dot(p2[W3:3 * W3, :], wide(MA + 2 * dx))
-        return carry
-
-    def mid_a_halo(dx, carry):
-        left = jnp.concatenate([p2[:HALF, :], p2[HALF:LANE, :]], axis=1)
-        add_rows(dx, dot(left, jnp.concatenate([wide(MA + 6 + 2 * dx), wide(MA + 12 + 2 * dx)], axis=0)))
-        return carry
-
-    wait_units(MA, MB)
-    lax.fori_loop(0, 3, mid_a_own, 0)
     halo_wait(p2, W3, 2, 3)
-    lax.fori_loop(0, 3, mid_a_halo, 0)
+    left = cat_lanes([p2[:HALF, :], p2[HALF:LANE, :]])
+    for dx in TAPS:
+        add_rows(dx, dot(left, cat_rows([wide(MA + 6 + 2 * dx), wide(MA + 12 + 2 * dx)])))
     finish_level3(4, act3, W3)
     halo_start(act3, W3, 2, 5)
     refill((MA, MB))
@@ -503,10 +521,10 @@
     for group, dy in enumerate(ROWS):
         def mid_b(dx, carry):
             first = MB + (group * 3 + dx) * SIDE
-            for part in range(SIDE):
+            for part in QUAD:
                 slot = slot_of(first + part)
                 pltpu.make_async_copy(h_e2b.at[0], ring.at[slot], sem_r.at[slot]).wait()
-            value = dot(act3[dy * W3:dy * W3 + HALF, :], jnp.concatenate([wide(first), wide(first + 2)], axis=0))
+            value = dot(act3[dy * W3:dy * W3 + HALF, :], cat_rows([wide(first), wide(first + 2)]))
             if group:
                 add_rows(dx, value)
             else:
@@ -520,13 +538,13 @@
     finish_level3(5, mid, 0)
 
     wait_units(UP2, D2A)
-    for tap in range(SIDE):
+    for tap in QUAD:
         p, q = tap // 2, tap % 2
         left = mid[...]
         for a, b in NTILES:
-            right = jnp.concatenate([ring[(UP2 + 2 * tap + part) % RING, :, a:b] for part in range(2)], axis=0)
+            right = cat_rows(ring[(UP2 + 2 * tap + part) % RING, :, a:b] for part in PAIR)
             part = dot(left, right)
-            for i in range(2):
+            for i in PAIR:
                 for c0 in range(a, b, LANE):
                     up_f32[pl.ds(c0 * 2 + (2 * i + p) * HALF + q, W3, stride=2), :] = part[W3 * i:W3 * i + W3, c0 - a:c0 - a + LANE]
     for block in range(5):
@@ -535,34 +553,17 @@
     refill((UP2, D2A))
     halo_wait(s2, HALF, SIDE, 4)
 
-    def dec2a(ref, first, dx):
-        left = stack_rows(ref, TILE, HALF)
-        for a, b in NTILES:
-            right = jnp.concatenate([ring[slot_of(first + dx * 3 + dy), :, a:b] for dy in TAPS], axis=0)
-            yield a, b, dot(left, right)
-
-    def dec2a_skip(dx, carry):
-        for a, b, value in dec2a(s2, D2A, dx):
-            pl2[dx, SUB:END, a:b] = value
-        return carry
-
-    def dec2a_up(dx, carry):
-        for a, b, value in dec2a(u2, D2A + TAP9, dx):
-            pl2[dx, SUB:END, a:b] = pl2[dx, SUB:END, a:b] + value
-        return carry
-
     wait_units(D2A, D2A + TAP9)
-    lax.fori_loop(0, 3, dec2a_skip, 0)
+    level2_taps(stack_rows(s2, TILE, HALF), unit_rows(D2A))
     refill((D2A, D2A + TAP9))
     wait_units(D2A + TAP9, D2B)
     halo_wait(u2, HALF, SIDE, 6)
-    lax.fori_loop(0, 3, dec2a_up, 0)
+    level2_taps(stack_rows(u2, TILE, HALF), unit_rows(D2A + TAP9), add=True)
     refill((D2A + TAP9, D2B))
     finish_level2(6, store_level2(act4, HALF))
     halo_start(act4, HALF, 4, 7)
     wait_units(D2B, UP1)
-    halo_wait(act4, HALF, 4, 7)
-    conv640(act4, lambda dx: [slot_of(D2B + dx * 3 + dy) for dy in TAPS])
+    conv640(act4, D2B, 7)
     finish_level2(7, store_level2(d2, 0))
 
     def half1(tap):
@@ -570,13 +571,13 @@
 
     refill((D2B, UP1))
     wait_units(UP1, D1A)
-    for tap in range(SIDE):
+    for tap in QUAD:
         p, q = tap // 2, tap % 2
         left = d2[...]
-        up = lax.dot_general(left, ring[(UP1 + tap // 2) % RING, half1(tap), :], (((1,), (1,)), ((), ())), preferred_element_type=F32)
+        up = dot_t(left, ring[(UP1 + tap // 2) % RING, half1(tap), :])
         for a, b in ((0, TILE), (TILE, C1)):
             part = up[:, a:b]
-            for i in range(SIDE):
+            for i in QUAD:
                 for c0 in range(a, b, LANE):
                     c1 = min(b, c0 + LANE)
                     up_f32[pl.ds(c0 * SUB + (2 * i + p) * LANE + q, HALF, stride=2), :c1 - c0] = part[HALF * i:HALF * i + HALF, c0 - a:c1 - a]
@@ -601,23 +602,20 @@
     build_tail(v_e1b, 0, t_e1b)
 
     def finish_head(i, pieces):
-        value = jnp.concatenate([piece.astype(BF16) for piece in pieces], axis=1)
-        head = lax.dot_general(w_out[...].astype(BF16), value, (((1,), (1,)), ((), ())), preferred_element_type=F32)
+        head = dot_t(w_out[...].astype(BF16), cat_lanes(piece.astype(BF16) for piece in pieces))
         ys[pl.ds(i, 1)] = head[None]
 
     conv_narrow(act5, TAP9, finish_head, (1, 1))
     halo_wait(act5, LANE, SUB, 9)
     conv_narrow(act5, TAP9, finish_head, (0, 3))
 
-    lanes8 = lax.broadcasted_iota(jnp.int32, (SUB, LANE), 1)
-    sub8 = lax.broadcasted_iota(jnp.int32, (SUB, LANE), 0)
-    for c in range(SIDE):
+    for c in QUAD:
         packed = jnp.zeros((SUB, LANE), F32)
         for y in range(SUB):
             line = ys[y // 2, :, (y % 2) * LANE:(y % 2) * LANE + LANE]
             slot = y % 4
             shift = (W3 * slot - W3 * c) % LANE
-            line = line if shift == 0 else pltpu.roll(line, shift, 1)
+            line = turn(line, shift)
             if y >= 4:
                 line = pltpu.roll(line, 4, 0)
             place = AND(AND(lanes8 >= W3 * slot, lanes8 < W3 * slot + W3), (sub8 >= 4) if y >= 4 else (sub8 < 4))
@@ -627,7 +625,7 @@
     def y_copy(c):
         return remote(ysend.at[c], yrecv.at[k_me], y_send.at[c], y_recv.at[k_me], c, col)
 
-    for c in range(SIDE):
+    for c in QUAD:
         here = is_me(c, col)
 
         @pl.when(NOT(here))
@@ -638,26 +636,30 @@
         def _():
             yrecv[pl.ds(k_me, 1)] = ysend[c][None]
 
-    for k in range(SIDE):
+    for k in QUAD:
         from_col, from_row = owner(4 * row + k)
 
         @pl.when(NOT(is_me(from_col, from_row)))
         def _():
             remote(ysend.at[0], yrecv.at[k], y_send.at[0], y_recv.at[k], col, row).wait_recv()
 
-    for c in range(SIDE):
+    for c in QUAD:
         @pl.when(NOT(is_me(c, col)))
         def _():
             y_copy(c).wait_send()
 
-    out_ref[...] = yrecv[...]
+    for k in QUAD:
+        for low in QUAD:
+            line = turn(yrecv[k], (LANE - low * W3) % LANE)
+            for high in PAIR:
+                out_ref[k * SUB + high * SIDE + low] = line[high * SIDE:high * SIDE + SIDE, :W3]
 
 
 def network(x, w_e1a, w_head, *rest):
     vmem = pl.BlockSpec(memory_space=pltpu.VMEM)
     hbm = pl.BlockSpec(memory_space=pl.ANY)
     dma = pltpu.SemaphoreType.DMA
-    scratch = [pltpu.VMEM(shape, F32) for shape in ((SIDE, STRIPS, LANE), (SIDE, SUB, LANE), (TILE, LANE))]
+    scratch = [pltpu.VMEM(shape, F32) for shape in ((5 * SUB, SUB, LANE), (5, SUB, LANE), (SIDE, 2, SUB, LANE), (SIDE, 1, SUB, LANE), (TILE, LANE))]
     level1, level2 = 10 * LANE, 6 * HALF
     scratch += [pltpu.VMEM(shape, BF16) for shape in (
         (level1, C1P), (level1, C2), (level2, C1P), (level2, C2), (level2, C2), (LANE, C2), (LANE, C3), (HALF, C3),
@@ -670,7 +672,7 @@
     scratch += [dma(shape) for shape in ((3,), (RING,), (SIDE,), (SIDE,), (2,), (SIDE,), (10, 2), (10, 2), (SIDE,), (SIDE,))]
     return pl.pallas_call(
         kernel,
-        out_shape=jax.ShapeDtypeStruct((SIDE, SUB, LANE), F32),
+        out_shape=jax.ShapeDtypeStruct((W3, SIDE, W3), F32),
         in_specs=[vmem] * 13 + [hbm] * 11,
         out_specs=vmem,
         scratch_shapes=scratch,
@@ -686,8 +688,6 @@
         (w_enc1a, b_enc1a, w_enc1b, b_enc1b, w_enc2a, b_enc2a, w_enc2b, b_enc2b,
          w_mid_a, b_mid_a, w_mid_b, b_mid_b, w_up2, w_dec2a, b_dec2a, w_dec2b, b_dec2b,
          w_up1, w_dec1a, b_dec1a, w_dec1b, b_dec1b, w_head, b_head) = params
-        x = jnp.transpose(tile, (0, 2, 1)).reshape(W3, LANE).astype(F32)
-        x = jnp.pad(x, ((2, 6), (0, 0)))
         biases = (b_enc1a, b_enc1b, b_enc2a, b_enc2b, b_mid_a, b_mid_b, b_dec2a, b_dec2b, b_dec1a, b_dec1b)
 
         def taps(weight):
@@ -698,9 +698,8 @@
 
         weights = [taps(w) for w in (w_enc1b, w_enc2a, w_enc2b, w_mid_a, w_mid_b, w_up2, w_dec2a, w_dec2b)]
         weights += [turned(w_up1), turned(w_dec1a), taps(w_dec1b)]
-        packed = network(x, taps(w_enc1a), w_head.T, *biases, *weights)
-        out = packed.reshape(4, 2, 4, 4, W3).transpose(0, 1, 3, 4, 2).reshape(W3, W3, 4)
-        return out + b_head
+        packed = network(jnp.transpose(tile, (0, 2, 1)), taps(w_enc1a), w_head.T, *biases, *weights)
+        return jnp.transpose(packed, (0, 2, 1)) + b_head
 
     def program(image, *params):
         mapped = jax.shard_map(device_body, mesh=mesh, in_specs=(tile_spec,) + tuple([P()] * len(params)), out_specs=tile_spec, check_vma=False)

time: 77.8 us -> 72.3 us (0.929)
  Pallas kernels: 73.8 us -> 70.3 us
  local copies, waits for them, and re-layouts: 1.67 us -> 0 us
    pallas_call x1, Pallas kernels: 73.8 us -> 70.3 us  [network(): pl.pallas_call(kernel, out_shape=jax.ShapeDtypeStruct((W3, SIDE, W3), F32...]
    convert_element_type x1 -> x0, local copies, waits for them, and re-layouts: 0.85 us -> none  [device_body(): x = jnp.transpose(tile, (0, 2, 1)).reshape(W3, LANE).astype(F32)]
    reshape x1 -> x0, local copies, waits for them, and re-layouts: 0.81 us -> none  [device_body(): packed.reshape(4, 2, 4, 4, W3).transpose(0, 1, 3, 4, 2).reshape(W3, W3, 4)]
where the time goes in v2:
time: 72.3 us; the launch traced here: 71.9 us
  Pallas kernels  70.3 us (97%)
  other arithmetic  1.55 us (2%)
    pallas_call x1, Pallas kernels, network(): pl.pallas_call(kernel, out_shape=jax.ShapeDtypeStruct((W3, SIDE, W3), F32...  70.3 us
    add x1, other arithmetic, device_body(): return jnp.transpose(packed, (0, 2, 1)) + b_head  1.55 us

profile of v2, /device:TPU:1, one launch (start us, length us, event | category | flops | bytes accessed | tf_op | source)
XLA Modules:
  0.0 71.9 jit_solution(6649028234861532765)
XLA Ops:
  0.0 70.3 %unet.1 = f32[32,4,32]{2,1,0:T(4,128)} custom-call(bf16[32,4,32]{2,1,0:T(4,128)(2,1)} %bitcast.31, bf16[9,4,320]{2,1,0:T(4,128)(2,1)} %bitcast.32, bf16[4,320]{1,0:T(4,128)(2,1)} %bitcast.33, f32[320]{0:T(512)} %refs_0_.1, f32[320]{0:T(512)} %refs_1_.1, f32[640]{0:T(1024)} %refs_2_.1, f32[640]{0:T(1024)} %refs_3_.1, f32[1280]{0:T(1024)} %refs_4_.1, ...), custom_call_target="tpu_custom_call" | custom-call | tf_op jit(solution)/shard_map/unet/pallas_call | solution.py:673
  70.3 1.5 %add_bitcast_fusion = f32[32,32,4]{1,2,0:T(4,128)} fusion(f32[32,4,32]{2,1,0:T(4,128)} %unet.1, f32[4]{0:T(128)} %param.49), kind=kLoop, calls=%fused_computation | loop fusion | flops 4096 | bytes 32784 | tf_op jit(solution)/shard_map/add | solution.py:702

commit v3 on v2

--- a/solution.py
+++ b/solution.py
@@ -20,7 +20,7 @@
 PAIR = range(2)
 QUAD = range(SIDE)
 TAP9 = 9
-RING = 50
+RING = 47
 E2B, MA, MB, UP2, D2A, D2B, UP1, D1A, UNITS = 0, 9, 27, 63, 71, 89, 98, 100, 105
 ROWS = (1, 0, 2)
 NOT = jnp.logical_not
@@ -139,7 +139,7 @@
 
     cp_e1b.start()
     cp_e2a.start()
-    for index in range(RING):
+    for index in range(MA):
         unit(index).start()
 
     bias[...] = jnp.zeros_like(bias)
@@ -166,6 +166,19 @@
     lax.fori_loop(0, 5, pack, 0)
     pl.semaphore_wait(barrier, LAST)
 
+    def build_tail(weights, base, tail):
+        def body(dy, carry):
+            parts = [weights[dy * 3 + dx, base:base + C1, TILE:C1].astype(F32) for dx in TAPS]
+            zero = jnp.zeros((C1, HALF), F32)
+            pair = cat_lanes(parts[:2])
+            last = cat_lanes([parts[2], zero])
+            tail[dy, :, :LANE] = pair.astype(BF16)
+            tail[dy, :, LANE:TILE] = last.astype(BF16)
+            return carry
+
+        lax.fori_loop(0, 3, body, 0)
+
+
     def is_me(strip_col, strip_row):
         return AND(strip_col == col, strip_row == row)
 
@@ -201,6 +214,11 @@
         @pl.when(AND(allowed, here))
         def _():
             xh[pl.ds(col, 1)] = xs[first:first + 1][None]
+
+    cp_e1b.wait()
+    build_tail(v_e1b, 0, t_e1b)
+    for index in range(MA, RING):
+        unit(index).start()
 
     for c in QUAD:
         @pl.when(NOT(is_me(c, row) & (row == col)))
@@ -313,18 +331,6 @@
             to_up.wait_recv()
             to_down.wait_send()
 
-    def build_tail(weights, base, tail):
-        def body(dy, carry):
-            parts = [weights[dy * 3 + dx, base:base + C1, TILE:C1].astype(F32) for dx in TAPS]
-            zero = jnp.zeros((C1, HALF), F32)
-            pair = cat_lanes(parts[:2])
-            last = cat_lanes([parts[2], zero])
-            tail[dy, :, :LANE] = pair.astype(BF16)
-            tail[dy, :, LANE:TILE] = last.astype(BF16)
-            return carry
-
-        lax.fori_loop(0, 3, body, 0)
-
     def narrow_lhs(ref, start, rows, width):
         mains = [ref[pl.ds(start + dy * width, rows), :TILE] for dy in TAPS]
         tails = [ref[pl.ds(start + dy * width, rows), TILE:C1P] for dy in TAPS]
@@ -348,59 +354,52 @@
         return slice(block * LANE, block * LANE + LANE)
 
     def conv_narrow(ref, bias_row, finish, chunks):
-        def chunk(step, carry):
-            i = chunks[0] + step * chunks[1]
-            start = pl.multiple_of(i * TILE, TILE)
-            left = narrow_lhs(ref, start, TILE, LANE)
+        for side, i in enumerate(chunks):
+            left = narrow_lhs(ref, i * TILE, TILE, LANE)
             for dx in TAPS:
-                pm[dx, SUB:END, :] = dot(left, narrow_rhs(lambda dy, a, b: v_e1b[dy * 3 + dx, a:b, :TILE]))
-            pt[SUB:END, :] = dot(left, narrow_rhs(lambda dy, a, b: t_e1b[dy, a:b, :]))
+                pm[side, dx, SUB:END, :] = dot(left, narrow_rhs(lambda dy, a, b: v_e1b[dy * 3 + dx, a:b, :TILE]))
+            pt[side, SUB:END, :] = dot(left, narrow_rhs(lambda dy, a, b: t_e1b[dy, a:b, :]))
+        for side, i in enumerate(chunks):
             pieces = []
             for block in PAIR:
                 lanes = blocks_of(block)
-                value = shifted(pm, lambda dx: (dx,), pm[1, SUB:END, lanes], (lanes, lanes))
+                value = shifted(pm, lambda dx: (side, dx), pm[side, 1, SUB:END, lanes], (lanes, lanes))
                 pieces.append(relu(value + bias[bias_row:bias_row + 1, lanes]))
-            value = shifted(pt, lambda dx: (), turn(pt[SUB:END, :LANE]), (blocks_of(0), blocks_of(1)))
+            value = shifted(pt, lambda dx: (side,), turn(pt[side, SUB:END, :LANE]), (blocks_of(0), blocks_of(1)))
             value = relu(value + bias[bias_row:bias_row + 1, TILE:C1P])
             pieces.append(jnp.where(low_half, value, 0.0))
             finish(i, pieces)
-            return carry
-
-        lax.fori_loop(0, 2, chunk, 0)
 
     def conv_cat(bias_row, finish, chunks):
-        def chunk(step, carry):
-            i = chunks[0] + step * chunks[1]
-            start = pl.multiple_of(i * TILE, TILE)
+        for side, i in enumerate(chunks):
+            start = i * TILE
             left = cat_lanes(cat1[pl.ds(start + dy * LANE, TILE), :] for dy in TAPS)
             right = cat_lanes(cat_rows(d1a_tap(dy * 3 + dx) for dx in TAPS) for dy in TAPS)
-            pd1[SUB:END, :3 * C1] = dot_t(left, right)
-            turned = [turn(pd1[SUB:END, blocks_of(2 + block)]) for block in TAPS]
+            pd1[side, SUB:END, :3 * C1] = dot_t(left, right)
+        for side, i in enumerate(chunks):
+            turned = [turn(pd1[side, SUB:END, blocks_of(2 + block)]) for block in TAPS]
             pieces = []
             for block in TAPS:
                 middle = turned[block] if block == 2 else jnp.where(low_half, turned[block], turned[block + 1])
-                value = shifted(pd1, lambda dx: (), middle, (blocks_of(block), blocks_of(5 + block) if block < 2 else slice(896, 1024)))
+                value = shifted(pd1, lambda dx: (side,), middle, (blocks_of(block), blocks_of(5 + block) if block < 2 else slice(896, 1024)))
                 value = relu(value + bias[bias_row:bias_row + 1, blocks_of(block)])
                 pieces.append(value if block < 2 else jnp.where(low_half, value, 0.0))
             finish(i, pieces)
-            return carry
-
-        lax.fori_loop(0, 2, chunk, 0)
 
     def store_level1(ref):
         def finish(i, pieces):
-            start = pl.multiple_of(LANE + i * TILE, LANE)
+            start = LANE + i * TILE
             for block in range(3):
                 ref[pl.ds(start, TILE), block * LANE:block * LANE + LANE] = pieces[block].astype(BF16)
         return finish
 
     def finish_s1(i, pieces):
-        at = pl.ds(pl.multiple_of(LANE + i * TILE, LANE), TILE)
+        at = pl.ds(LANE + i * TILE, TILE)
         turned = [turn(piece) for piece in pieces]
         cat1[at, TILE:C1P] = jnp.where(low_half, 0.0, turned[0]).astype(BF16)
         for block in PAIR:
             cat1[at, blocks_of(3 + block)] = jnp.where(low_half, turned[block], turned[block + 1]).astype(BF16)
-        start = pl.multiple_of(HALF + i * HALF, HALF)
+        start = HALF + i * HALF
         for block in range(3):
             pool[:LANE, :] = jnp.maximum(pieces[block][:LANE], pieces[block][LANE:TILE])
             pooled = jnp.maximum(pool[pl.ds(0, HALF, stride=2), :], pool[pl.ds(1, HALF, stride=2), :])
@@ -408,12 +407,10 @@
 
     S1_LANES = pl.ds(C1P, TILE)
     U1_LANES = pl.ds(0, C1P)
-    cp_e1b.wait()
-    build_tail(v_e1b, 0, t_e1b)
     conv_narrow(act1, 1, finish_s1, (0, 3))
     halo_start(p1, HALF, SIDE, 0)
     halo_start(cat1, LANE, SUB, 1, S1_LANES)
-    conv_narrow(act1, 1, finish_s1, (1, 1))
+    conv_narrow(act1, 1, finish_s1, (1, 2))
     cp_d1b.start()
 
     x_index2 = column_index(TILE, HALF)
@@ -510,6 +507,8 @@
     wait_units(MA, MB)
     for dx in TAPS:
         pl3[dx, SUB:72, :] = dot(p2[W3:3 * W3, :], wide(MA + 2 * dx))
+    cp_d1b.wait()
+    build_tail(v_e1b, 0, t_e1b)
     halo_wait(p2, W3, 2, 3)
     left = cat_lanes([p2[:HALF, :], p2[HALF:LANE, :]])
     for dx in TAPS:
@@ -593,19 +592,17 @@
         return ring[(D1A + tap // 2) % RING, half1(tap), :]
 
     wait_units(D1A, UNITS)
-    conv_cat(8, store_level1(act5), (1, 1))
+    conv_cat(8, store_level1(act5), (1, 2))
     halo_wait(cat1, LANE, SUB, 1, S1_LANES)
     halo_wait(cat1, LANE, SUB, 8, U1_LANES)
     conv_cat(8, store_level1(act5), (0, 3))
     halo_start(act5, LANE, SUB, 9)
-    cp_d1b.wait()
-    build_tail(v_e1b, 0, t_e1b)
 
     def finish_head(i, pieces):
         head = dot_t(w_out[...].astype(BF16), cat_lanes(piece.astype(BF16) for piece in pieces))
         ys[pl.ds(i, 1)] = head[None]
 
-    conv_narrow(act5, TAP9, finish_head, (1, 1))
+    conv_narrow(act5, TAP9, finish_head, (1, 2))
     halo_wait(act5, LANE, SUB, 9)
     conv_narrow(act5, TAP9, finish_head, (0, 3))
 
@@ -667,7 +664,7 @@
         (TAP9, C1, C1), (TAP9, C1, C2), (3, C1, TILE), (RING, C2, C2))]
     scratch += [pltpu.VMEM(shape, F32) for shape in (
         (10, C3), (48, C1P), (SUB, C1P),
-        (3, MARGIN, TILE), (MARGIN, TILE), (3, MARGIN, C2), (3, 80, C3), (MARGIN, 1024),
+        (2, 3, MARGIN, TILE), (2, MARGIN, TILE), (3, MARGIN, C2), (3, 80, C3), (2, MARGIN, 1024),
         (LANE, LANE), (3072, LANE), (SIDE, SUB, TILE), (SIDE, SUB, LANE), (SIDE, SUB, LANE))]
     scratch += [dma(shape) for shape in ((3,), (RING,), (SIDE,), (SIDE,), (2,), (SIDE,), (10, 2), (10, 2), (SIDE,), (SIDE,))]
     return pl.pallas_call(

time: 72.3 us -> 66.2 us (0.916)
  Pallas kernels: 70.3 us -> 64.4 us
    pallas_call x1, Pallas kernels: 70.3 us -> 64.4 us  [network(): pl.pallas_call(kernel, out_shape=jax.ShapeDtypeStruct((W3, SIDE, W3), F32...]
where the time goes in v3:
time: 66.2 us; the launch traced here: 66 us
  Pallas kernels  64.4 us (97%)
  other arithmetic  1.55 us (2%)
    pallas_call x1, Pallas kernels, network(): pl.pallas_call(kernel, out_shape=jax.ShapeDtypeStruct((W3, SIDE, W3), F32...  64.4 us
    add x1, other arithmetic, device_body(): return jnp.transpose(packed, (0, 2, 1)) + b_head  1.55 us

profile of v3, /device:TPU:1, one launch (start us, length us, event | category | flops | bytes accessed | tf_op | source)
XLA Modules:
  0.0 66.0 jit_solution(1915050618852415090)
XLA Ops:
  0.0 64.4 %unet.1 = f32[32,4,32]{2,1,0:T(4,128)} custom-call(bf16[32,4,32]{2,1,0:T(4,128)(2,1)} %bitcast.31, bf16[9,4,320]{2,1,0:T(4,128)(2,1)} %bitcast.32, bf16[4,320]{1,0:T(4,128)(2,1)} %bitcast.33, f32[320]{0:T(512)} %refs_0_.1, f32[320]{0:T(512)} %refs_1_.1, f32[640]{0:T(1024)} %refs_2_.1, f32[640]{0:T(1024)} %refs_3_.1, f32[1280]{0:T(1024)} %refs_4_.1, ...), custom_call_target="tpu_custom_call" | custom-call | tf_op jit(solution)/shard_map/unet/pallas_call | solution.py:670
  64.4 1.5 %add_bitcast_fusion = f32[32,32,4]{1,2,0:T(4,128)} fusion(f32[32,4,32]{2,1,0:T(4,128)} %unet.1, f32[4]{0:T(128)} %param.49), kind=kLoop, calls=%fused_computation | loop fusion | flops 4096 | bytes 32784 | tf_op jit(solution)/shard_map/add | solution.py:699

commit v4 on v3

--- a/solution.py
+++ b/solution.py
@@ -307,26 +307,34 @@
                          e_send.at[index, 1], e_recv.at[index, 1], down_col, down_row)
         return to_up, to_down
 
-    def halo_start(ref, width, height, index, lanes=slice(None)):
+    odd = k_me % 2 == 1
+    even = NOT(odd)
+    far = (k_me % 2) * 3
+    near = 3 - far
+    ANY = (True, True)
+    FAR = (even, odd)
+    NEAR = (odd, even)
+
+    def halo_start(ref, width, height, index, lanes=slice(None), sides=ANY):
         to_up, to_down = halo_copies(ref, width, height, index, lanes)
 
-        @pl.when(me > 0)
+        @pl.when(AND(me > 0, sides[0]))
         def _():
             to_up.start()
 
-        @pl.when(me < LAST)
+        @pl.when(AND(me < LAST, sides[1]))
         def _():
             to_down.start()
 
-    def halo_wait(ref, width, height, index, lanes=slice(None)):
+    def halo_wait(ref, width, height, index, lanes=slice(None), sides=ANY):
         to_up, to_down = halo_copies(ref, width, height, index, lanes)
 
-        @pl.when(me > 0)
+        @pl.when(AND(me > 0, sides[0]))
         def _():
             to_down.wait_recv()
             to_up.wait_send()
 
-        @pl.when(me < LAST)
+        @pl.when(AND(me < LAST, sides[1]))
         def _():
             to_up.wait_recv()
             to_down.wait_send()
@@ -350,12 +358,15 @@
         first = left + jnp.where(not_first, ref[plane(0) + (slice(7, 263), right[0])], 0.0)
         return first + jnp.where(not_last, ref[plane(2) + (slice(9, 265), right[1])], 0.0)
 
+    def scaled(i, step):
+        return i * step if isinstance(i, int) else pl.multiple_of(i * step, step)
+
     def blocks_of(block):
         return slice(block * LANE, block * LANE + LANE)
 
     def conv_narrow(ref, bias_row, finish, chunks):
         for side, i in enumerate(chunks):
-            left = narrow_lhs(ref, i * TILE, TILE, LANE)
+            left = narrow_lhs(ref, scaled(i, TILE), TILE, LANE)
             for dx in TAPS:
                 pm[side, dx, SUB:END, :] = dot(left, narrow_rhs(lambda dy, a, b: v_e1b[dy * 3 + dx, a:b, :TILE]))
             pt[side, SUB:END, :] = dot(left, narrow_rhs(lambda dy, a, b: t_e1b[dy, a:b, :]))
@@ -372,7 +383,7 @@
 
     def conv_cat(bias_row, finish, chunks):
         for side, i in enumerate(chunks):
-            start = i * TILE
+            start = scaled(i, TILE)
             left = cat_lanes(cat1[pl.ds(start + dy * LANE, TILE), :] for dy in TAPS)
             right = cat_lanes(cat_rows(d1a_tap(dy * 3 + dx) for dx in TAPS) for dy in TAPS)
             pd1[side, SUB:END, :3 * C1] = dot_t(left, right)
@@ -388,18 +399,18 @@
 
     def store_level1(ref):
         def finish(i, pieces):
-            start = LANE + i * TILE
+            start = LANE + scaled(i, TILE)
             for block in range(3):
                 ref[pl.ds(start, TILE), block * LANE:block * LANE + LANE] = pieces[block].astype(BF16)
         return finish
 
     def finish_s1(i, pieces):
-        at = pl.ds(LANE + i * TILE, TILE)
+        at = pl.ds(LANE + scaled(i, TILE), TILE)
         turned = [turn(piece) for piece in pieces]
         cat1[at, TILE:C1P] = jnp.where(low_half, 0.0, turned[0]).astype(BF16)
         for block in PAIR:
             cat1[at, blocks_of(3 + block)] = jnp.where(low_half, turned[block], turned[block + 1]).astype(BF16)
-        start = HALF + i * HALF
+        start = HALF + scaled(i, HALF)
         for block in range(3):
             pool[:LANE, :] = jnp.maximum(pieces[block][:LANE], pieces[block][LANE:TILE])
             pooled = jnp.maximum(pool[pl.ds(0, HALF, stride=2), :], pool[pl.ds(1, HALF, stride=2), :])
@@ -407,8 +418,10 @@
 
     S1_LANES = pl.ds(C1P, TILE)
     U1_LANES = pl.ds(0, C1P)
-    conv_narrow(act1, 1, finish_s1, (0, 3))
-    halo_start(p1, HALF, SIDE, 0)
+    conv_narrow(act1, 1, finish_s1, (far,))
+    halo_start(p1, HALF, SIDE, 0, sides=FAR)
+    conv_narrow(act1, 1, finish_s1, (near,))
+    halo_start(p1, HALF, SIDE, 0, sides=NEAR)
     halo_start(cat1, LANE, SUB, 1, S1_LANES)
     conv_narrow(act1, 1, finish_s1, (1, 2))
     cp_d1b.start()
@@ -469,8 +482,8 @@
     finish_level2(2, store_level2(act2, HALF))
     halo_start(act2, HALF, 4, 2)
 
-    def conv640(ref, first, index):
-        level2_taps(ref[HALF:HALF + TILE, :], unit_rows(first, (1,)))
+    def conv640(ref, first, index, add=False):
+        level2_taps(ref[HALF:HALF + TILE, :], unit_rows(first, (1,)), add)
         halo_wait(ref, HALF, SIDE, index)
         level2_taps(stack_rows(ref, TILE, HALF, (0, 2)), unit_rows(first, (0, 2)), add=True)
 
@@ -496,7 +509,7 @@
         lax.fori_loop(0, 10, body, 0)
 
     def slot_of(index):
-        return lax.rem(index, RING)
+        return index % RING
 
     def wide(first):
         return cat_lanes([ring[slot_of(first)], ring[slot_of(first + 1)]])
@@ -518,22 +531,19 @@
     refill((MA, MB))
 
     for group, dy in enumerate(ROWS):
-        def mid_b(dx, carry):
-            first = MB + (group * 3 + dx) * SIDE
-            for part in QUAD:
-                slot = slot_of(first + part)
-                pltpu.make_async_copy(h_e2b.at[0], ring.at[slot], sem_r.at[slot]).wait()
-            value = dot(act3[dy * W3:dy * W3 + HALF, :], cat_rows([wide(first), wide(first + 2)]))
+        if group == 1:
+            halo_wait(act3, W3, 2, 5)
+        begin = MB + group * 12
+        wait_units(begin, begin + 12)
+        left = act3[dy * W3:dy * W3 + HALF, :]
+        for dx in TAPS:
+            first = begin + dx * SIDE
+            value = dot(left, cat_rows([wide(first), wide(first + 2)]))
             if group:
                 add_rows(dx, value)
             else:
                 pl3[dx, SUB:72, :] = value
-            return carry
-
-        if group == 1:
-            halo_wait(act3, W3, 2, 5)
-        lax.fori_loop(0, 3, mid_b, 0)
-        refill((MB + group * 12, MB + group * 12 + 12))
+        refill((begin, begin + 12))
     finish_level3(5, mid, 0)
 
     wait_units(UP2, D2A)
@@ -556,8 +566,7 @@
     level2_taps(stack_rows(s2, TILE, HALF), unit_rows(D2A))
     refill((D2A, D2A + TAP9))
     wait_units(D2A + TAP9, D2B)
-    halo_wait(u2, HALF, SIDE, 6)
-    level2_taps(stack_rows(u2, TILE, HALF), unit_rows(D2A + TAP9), add=True)
+    conv640(u2, D2A + TAP9, 6, True)
     refill((D2A + TAP9, D2B))
     finish_level2(6, store_level2(act4, HALF))
     halo_start(act4, HALF, 4, 7)
@@ -594,17 +603,22 @@
     wait_units(D1A, UNITS)
     conv_cat(8, store_level1(act5), (1, 2))
     halo_wait(cat1, LANE, SUB, 1, S1_LANES)
-    halo_wait(cat1, LANE, SUB, 8, U1_LANES)
-    conv_cat(8, store_level1(act5), (0, 3))
-    halo_start(act5, LANE, SUB, 9)
+    halo_wait(cat1, LANE, SUB, 8, U1_LANES, NEAR)
+    conv_cat(8, store_level1(act5), (near,))
+    halo_start(act5, LANE, SUB, TAP9, sides=NEAR)
+    halo_wait(cat1, LANE, SUB, 8, U1_LANES, FAR)
+    conv_cat(8, store_level1(act5), (far,))
+    halo_start(act5, LANE, SUB, TAP9, sides=FAR)
 
     def finish_head(i, pieces):
         head = dot_t(w_out[...].astype(BF16), cat_lanes(piece.astype(BF16) for piece in pieces))
         ys[pl.ds(i, 1)] = head[None]
 
     conv_narrow(act5, TAP9, finish_head, (1, 2))
-    halo_wait(act5, LANE, SUB, 9)
-    conv_narrow(act5, TAP9, finish_head, (0, 3))
+    halo_wait(act5, LANE, SUB, TAP9, sides=NEAR)
+    conv_narrow(act5, TAP9, finish_head, (near,))
+    halo_wait(act5, LANE, SUB, TAP9, sides=FAR)
+    conv_narrow(act5, TAP9, finish_head, (far,))
 
     for c in QUAD:
         packed = jnp.zeros((SUB, LANE), F32)

time: 66.2 us -> 62.9 us (0.950)
  Pallas kernels: 64.4 us -> 61.1 us
    pallas_call x1, Pallas kernels: 64.4 us -> 61.1 us  [network(): pl.pallas_call(kernel, out_shape=jax.ShapeDtypeStruct((W3, SIDE, W3), F32...]
where the time goes in v4:
time: 62.9 us; the launch traced here: 62.6 us
  Pallas kernels  61.1 us (97%)
  other arithmetic  1.55 us (2%)
    pallas_call x1, Pallas kernels, network(): pl.pallas_call(kernel, out_shape=jax.ShapeDtypeStruct((W3, SIDE, W3), F32...  61.1 us
    add x1, other arithmetic, device_body(): return jnp.transpose(packed, (0, 2, 1)) + b_head  1.55 us

profile of v4, /device:TPU:1, one launch (start us, length us, event | category | flops | bytes accessed | tf_op | source)
XLA Modules:
  0.0 62.6 jit_solution(17338911388887851946)
XLA Ops:
  0.0 61.1 %unet.1 = f32[32,4,32]{2,1,0:T(4,128)} custom-call(bf16[32,4,32]{2,1,0:T(4,128)(2,1)} %bitcast.31, bf16[9,4,320]{2,1,0:T(4,128)(2,1)} %bitcast.32, bf16[4,320]{1,0:T(4,128)(2,1)} %bitcast.33, f32[320]{0:T(512)} %refs_0_.1, f32[320]{0:T(512)} %refs_1_.1, f32[640]{0:T(1024)} %refs_2_.1, f32[640]{0:T(1024)} %refs_3_.1, f32[1280]{0:T(1024)} %refs_4_.1, ...), custom_call_target="tpu_custom_call" | custom-call | tf_op jit(solution)/shard_map/unet/pallas_call | solution.py:684
  61.1 1.5 %add_bitcast_fusion = f32[32,32,4]{1,2,0:T(4,128)} fusion(f32[32,4,32]{2,1,0:T(4,128)} %unet.1, f32[4]{0:T(128)} %param.49), kind=kLoop, calls=%fused_computation | loop fusion | flops 4096 | bytes 32784 | tf_op jit(solution)/shard_map/add | solution.py:713

commit v5 on v4

--- a/solution.py
+++ b/solution.py
@@ -458,9 +458,18 @@
     def stack_rows(ref, rows, width, taps=TAPS):
         return cat_lanes(ref[dy * width:dy * width + rows, :] for dy in taps)
 
-    def level2_taps(left, weights, add=False):
+    def level2_taps(left, weights, add=False, groups=QUAD):
+        if groups is not QUAD:
+            left = cat_rows(left[group * HALF:group * HALF + HALF] for group in groups)
+
         def put(dx, lanes, value):
-            pl2[dx, SUB:END, lanes] = pl2[dx, SUB:END, lanes] + value if add else value
+            if groups is QUAD:
+                pl2[dx, SUB:END, lanes] = pl2[dx, SUB:END, lanes] + value if add else value
+                return
+            for part, group in enumerate(groups):
+                at = slice(SUB + group * HALF, SUB + group * HALF + HALF)
+                piece = value[part * HALF:part * HALF + HALF]
+                pl2[dx, at, lanes] = pl2[dx, at, lanes] + piece if add else piece
 
         for dx in TAPS:
             for first, last in NTILES[:2]:
@@ -477,15 +486,37 @@
     halo_wait(p1, HALF, 4, 0)
     cp_e2a.wait()
 
-    level2_taps(narrow_lhs(p1, 0, TILE, HALF),
-                lambda dx, lanes: narrow_rhs(lambda dy, r0, r1: v_e2a[dy * 3 + dx, r0:r1, lanes]))
-    finish_level2(2, store_level2(act2, HALF))
-    halo_start(act2, HALF, 4, 2)
-
-    def conv640(ref, first, index, add=False):
+    def finish_groups(bias_row, ref, groups):
+        def body(block, carry):
+            lanes = pl.ds(pl.multiple_of(block * LANE, LANE), LANE)
+            for group in groups:
+                at = SUB + group * HALF
+                value = pl2[1, at:at + HALF, lanes] + jnp.where(not_first2[:HALF], pl2[0, at - 1:at - 1 + HALF, lanes], 0.0)
+                value = value + jnp.where(not_last2[:HALF], pl2[2, at + 1:at + 1 + HALF, lanes], 0.0)
+                value = relu(value + bias[bias_row:bias_row + 1, lanes])
+                ref[(group + 1) * HALF:(group + 2) * HALF, lanes] = value.astype(BF16)
+            return carry
+
+        lax.fori_loop(0, 5, body, 0)
+
+    def edges_first(left, weights, add, bias_row, ref, index):
+        for groups in ((0, 3), (1, 2)):
+            level2_taps(left, weights, add, groups)
+            finish_groups(bias_row, ref, groups)
+            if 0 in groups:
+                halo_start(ref, HALF, SIDE, index)
+
+    edges_first(narrow_lhs(p1, 0, TILE, HALF),
+                lambda dx, lanes: narrow_rhs(lambda dy, r0, r1: v_e2a[dy * 3 + dx, r0:r1, lanes]), False, 2, act2, 2)
+
+    def conv640(ref, first, index, add=False, finish=None):
         level2_taps(ref[HALF:HALF + TILE, :], unit_rows(first, (1,)), add)
         halo_wait(ref, HALF, SIDE, index)
-        level2_taps(stack_rows(ref, TILE, HALF, (0, 2)), unit_rows(first, (0, 2)), add=True)
+        left = stack_rows(ref, TILE, HALF, (0, 2))
+        if finish is None:
+            level2_taps(left, unit_rows(first, (0, 2)), add=True)
+        else:
+            edges_first(left, unit_rows(first, (0, 2)), True, *finish)
 
     wait_units(E2B, MA)
     conv640(act2, E2B, 2)
@@ -566,10 +597,8 @@
     level2_taps(stack_rows(s2, TILE, HALF), unit_rows(D2A))
     refill((D2A, D2A + TAP9))
     wait_units(D2A + TAP9, D2B)
-    conv640(u2, D2A + TAP9, 6, True)
+    conv640(u2, D2A + TAP9, 6, True, (6, act4, 7))
     refill((D2A + TAP9, D2B))
-    finish_level2(6, store_level2(act4, HALF))
-    halo_start(act4, HALF, 4, 7)
     wait_units(D2B, UP1)
     conv640(act4, D2B, 7)
     finish_level2(7, store_level2(d2, 0))

time: 62.9 us -> 61.5 us (0.978)
  Pallas kernels: 61.1 us -> 59.7 us
    pallas_call x1, Pallas kernels: 61.1 us -> 59.7 us  [network(): pl.pallas_call(kernel, out_shape=jax.ShapeDtypeStruct((W3, SIDE, W3), F32...]
where the time goes in v5:
time: 61.5 us; the launch traced here: 61.3 us
  Pallas kernels  59.7 us (97%)
  other arithmetic  1.55 us (3%)
    pallas_call x1, Pallas kernels, network(): pl.pallas_call(kernel, out_shape=jax.ShapeDtypeStruct((W3, SIDE, W3), F32...  59.7 us
    add x1, other arithmetic, device_body(): return jnp.transpose(packed, (0, 2, 1)) + b_head  1.55 us

profile of v5, /device:TPU:1, one launch (start us, length us, event | category | flops | bytes accessed | tf_op | source)
XLA Modules:
  0.0 61.3 jit_solution(4888038839948864964)
XLA Ops:
  0.0 59.7 %unet.1 = f32[32,4,32]{2,1,0:T(4,128)} custom-call(bf16[32,4,32]{2,1,0:T(4,128)(2,1)} %bitcast.31, bf16[9,4,320]{2,1,0:T(4,128)(2,1)} %bitcast.32, bf16[4,320]{1,0:T(4,128)(2,1)} %bitcast.33, f32[320]{0:T(512)} %refs_0_.1, f32[320]{0:T(512)} %refs_1_.1, f32[640]{0:T(1024)} %refs_2_.1, f32[640]{0:T(1024)} %refs_3_.1, f32[1280]{0:T(1024)} %refs_4_.1, ...), custom_call_target="tpu_custom_call" | custom-call | tf_op jit(solution)/shard_map/unet/pallas_call | solution.py:713
  59.7 1.5 %add_bitcast_fusion = f32[32,32,4]{1,2,0:T(4,128)} fusion(f32[32,4,32]{2,1,0:T(4,128)} %unet.1, f32[4]{0:T(128)} %param.49), kind=kLoop, calls=%fused_computation | loop fusion | flops 4096 | bytes 32784 | tf_op jit(solution)/shard_map/add | solution.py:742

commit v6 on v5

--- a/solution.py
+++ b/solution.py
@@ -459,7 +459,7 @@
         return cat_lanes(ref[dy * width:dy * width + rows, :] for dy in taps)
 
     def level2_taps(left, weights, add=False, groups=QUAD):
-        if groups is not QUAD:
+        if groups is not QUAD and left.shape[0] == TILE:
             left = cat_rows(left[group * HALF:group * HALF + HALF] for group in groups)
 
         def put(dx, lanes, value):
@@ -511,10 +511,13 @@
 
     def conv640(ref, first, index, add=False, finish=None):
         level2_taps(ref[HALF:HALF + TILE, :], unit_rows(first, (1,)), add)
+        if finish is None:
+            inner = cat_lanes([ref[HALF:HALF + LANE, :], ref[3 * HALF:3 * HALF + LANE, :]])
+            level2_taps(inner, unit_rows(first, (0, 2)), True, (1, 2))
         halo_wait(ref, HALF, SIDE, index)
         left = stack_rows(ref, TILE, HALF, (0, 2))
         if finish is None:
-            level2_taps(left, unit_rows(first, (0, 2)), add=True)
+            level2_taps(left, unit_rows(first, (0, 2)), True, (0, 3))
         else:
             edges_first(left, unit_rows(first, (0, 2)), True, *finish)
 

time: 61.5 us -> 60.2 us (0.979)
  Pallas kernels: 59.7 us -> 58.4 us
    pallas_call x1, Pallas kernels: 59.7 us -> 58.4 us  [network(): pl.pallas_call(kernel, out_shape=jax.ShapeDtypeStruct((W3, SIDE, W3), F32...]
where the time goes in v6:
time: 60.2 us; the launch traced here: 60 us
  Pallas kernels  58.4 us (97%)
  other arithmetic  1.55 us (3%)
    pallas_call x1, Pallas kernels, network(): pl.pallas_call(kernel, out_shape=jax.ShapeDtypeStruct((W3, SIDE, W3), F32...  58.4 us
    add x1, other arithmetic, device_body(): return jnp.transpose(packed, (0, 2, 1)) + b_head  1.55 us

profile of v6, /device:TPU:1, one launch (start us, length us, event | category | flops | bytes accessed | tf_op | source)
XLA Modules:
  0.0 60.0 jit_solution(4615220874614893577)
XLA Ops:
  0.0 58.4 %unet.1 = f32[32,4,32]{2,1,0:T(4,128)} custom-call(bf16[32,4,32]{2,1,0:T(4,128)(2,1)} %bitcast.31, bf16[9,4,320]{2,1,0:T(4,128)(2,1)} %bitcast.32, bf16[4,320]{1,0:T(4,128)(2,1)} %bitcast.33, f32[320]{0:T(512)} %refs_0_.1, f32[320]{0:T(512)} %refs_1_.1, f32[640]{0:T(1024)} %refs_2_.1, f32[640]{0:T(1024)} %refs_3_.1, f32[1280]{0:T(1024)} %refs_4_.1, ...), custom_call_target="tpu_custom_call" | custom-call | tf_op jit(solution)/shard_map/unet/pallas_call | solution.py:716
  58.4 1.5 %add_bitcast_fusion = f32[32,32,4]{1,2,0:T(4,128)} fusion(f32[32,4,32]{2,1,0:T(4,128)} %unet.1, f32[4]{0:T(128)} %param.49), kind=kLoop, calls=%fused_computation | loop fusion | flops 4096 | bytes 32784 | tf_op jit(solution)/shard_map/add | solution.py:745
